TPU v7x, 32 devices: a whole 2x2x4 slice. The times are simulated.
32 devices in a mesh: fsdp: 32 (over z, y, x, core).
Axes of the slice: x: 2, y: 2, z: 4, core: 2. Of those that a mesh axis runs over, the one named last changes fastest.
Arguments:
- x_saved: bfloat16 [2, 32, 1536, 1280], P(None, 'fsdp')
- grad_out: bfloat16 [32, 1536, 1280], P('fsdp')
- x_next: bfloat16 [32, 1536, 1280], P('fsdp')
- w_up: bfloat16 [2, 1280, 5120], replicated
- w_down: bfloat16 [2, 5120, 1280], replicated
- gacc_up: float32 [2, 1280, 5120], P(None, 'fsdp')
- gacc_down: float32 [2, 5120, 1280], P(None, 'fsdp')
- master_up: float32 [2, 1280, 5120], P(None, 'fsdp')
- master_down: float32 [2, 5120, 1280], P(None, 'fsdp')
- mom1_up: float32 [2, 1280, 5120], P(None, 'fsdp')
- mom1_down: float32 [2, 5120, 1280], P(None, 'fsdp')
- mom2_up: float32 [2, 1280, 5120], P(None, 'fsdp')
- mom2_down: float32 [2, 5120, 1280], P(None, 'fsdp')
Outputs:
- output 1: bfloat16 [32, 1536, 1280], P('fsdp')
- output 2: float32 [2, 1280, 5120], P(None, 'fsdp')
- output 3: float32 [2, 5120, 1280], P(None, 'fsdp')
- output 4: float32 [2, 1280, 5120], P(None, 'fsdp')
- output 5: float32 [2, 5120, 1280], P(None, 'fsdp')
- output 6: float32 [2, 1280, 5120], P(None, 'fsdp')
- output 7: float32 [2, 5120, 1280], P(None, 'fsdp')
All inputs are finite; a program needn't handle non-finite values.
Results may differ from a plain program's by a relative error of at most 0.00841707.
Values are sent between devices in bfloat16 or wider.
A program may use at most 1 GiB of HBM per device.

v0:
```python
import math
import jax
import jax.numpy as jnp
from jax import lax
from jax.sharding import PartitionSpec as P

LEARN_RATE = 0.001
BETA_ONE = 0.9
BETA_TWO = 0.95
ADAM_EPS = 1e-8
WEIGHT_DECAY = 0.1
ADAM_STEP = 3
MICRO_STEPS = 2


def gelu_fn(pre_act):
    return jax.nn.gelu(pre_act, approximate=True)


def adamw_update(master_old, mom_one, mom_two, grad_clip):
    mom_one_new = BETA_ONE * mom_one + (1.0 - BETA_ONE) * grad_clip
    mom_two_new = BETA_TWO * mom_two + (1.0 - BETA_TWO) * grad_clip * grad_clip
    first_hat = mom_one_new / (1.0 - BETA_ONE ** ADAM_STEP)
    second_hat = mom_two_new / (1.0 - BETA_TWO ** ADAM_STEP)
    master_new = master_old - LEARN_RATE * (first_hat / (jnp.sqrt(second_hat) + ADAM_EPS) + WEIGHT_DECAY * master_old)
    return master_new, mom_one_new, mom_two_new


def reduce_rows(part_grad, n_dev):
    received = lax.all_to_all(part_grad, "fsdp", 0, 0, tiled=True)
    return jnp.sum(received.reshape(n_dev, -1, part_grad.shape[1]), axis=0, dtype=jnp.float32)


def backward_update(x_saved, grad_out, w_up, w_down, gacc_up, gacc_down, master_up, master_down, mom1_up, mom1_down, mom2_up, mom2_down, n_dev):
    layers, model_width, ff_width = w_up.shape
    clip_norm = 0.1 * math.sqrt(2 * layers * model_width * ff_width)
    x_tokens = x_saved.reshape(layers, -1, model_width)
    grad_cur = grad_out.reshape(-1, model_width)
    sums_up = []
    sums_down = []
    for layer_idx in range(layers - 1, -1, -1):
        x_in = x_tokens[layer_idx]
        pre_act = jnp.dot(x_in, w_up[layer_idx], preferred_element_type=jnp.float32)
        hidden_act, gelu_vjp = jax.vjp(gelu_fn, pre_act)
        d_act = lax.dot_general(grad_cur, w_down[layer_idx], (((1,), (1,)), ((), ())), preferred_element_type=jnp.float32)
        d_pre = gelu_vjp(d_act)[0].astype(jnp.bfloat16)
        part_down = lax.dot_general(hidden_act.astype(jnp.bfloat16), grad_cur, (((0,), (0,)), ((), ())), preferred_element_type=jnp.float32).astype(jnp.bfloat16)
        part_up = lax.dot_general(x_in, d_pre, (((0,), (0,)), ((), ())), preferred_element_type=jnp.float32).astype(jnp.bfloat16)
        if layer_idx > 0:
            grad_cur = (grad_cur.astype(jnp.float32) + lax.dot_general(d_pre, w_up[layer_idx], (((1,), (1,)), ((), ())), preferred_element_type=jnp.float32)).astype(jnp.bfloat16)
        sums_down.append(reduce_rows(part_down, n_dev))
        sums_up.append(reduce_rows(part_up, n_dev))
    grad_up = (gacc_up + jnp.stack(sums_up[::-1])) / MICRO_STEPS
    grad_down = (gacc_down + jnp.stack(sums_down[::-1])) / MICRO_STEPS
    local_sq = jnp.sum(grad_up * grad_up) + jnp.sum(grad_down * grad_down)
    clip_factor = jnp.minimum(1.0, clip_norm / jnp.sqrt(lax.psum(local_sq, "fsdp")))
    new_up = adamw_update(master_up, mom1_up, mom2_up, grad_up * clip_factor)
    new_down = adamw_update(master_down, mom1_down, mom2_down, grad_down * clip_factor)
    return new_up, new_down


def solution(mesh):
    n_dev = mesh.shape["fsdp"]
    rows_spec = P(None, "fsdp")

    def local_step(x_saved, grad_out, x_next, w_up, w_down, gacc_up, gacc_down, master_up, master_down, mom1_up, mom1_down, mom2_up, mom2_down):
        new_up, new_down = backward_update(x_saved, grad_out, w_up, w_down, gacc_up, gacc_down, master_up, master_down, mom1_up, mom1_down, mom2_up, mom2_down, n_dev)
        up_shard = new_up[0].astype(jnp.bfloat16)
        down_shard = new_down[0].astype(jnp.bfloat16)
        hidden_state = x_next.reshape(-1, x_next.shape[2])
        for layer_idx in range(up_shard.shape[0]):
            w_layer_up = lax.all_gather(up_shard[layer_idx], "fsdp", axis=0, tiled=True)
            w_layer_down = lax.all_gather(down_shard[layer_idx], "fsdp", axis=0, tiled=True)
            pre_act = jnp.dot(hidden_state, w_layer_up, preferred_element_type=jnp.float32)
            hidden_act = gelu_fn(pre_act).astype(jnp.bfloat16)
            hidden_state = (hidden_state.astype(jnp.float32) + jnp.dot(hidden_act, w_layer_down, preferred_element_type=jnp.float32)).astype(jnp.bfloat16)
        return (hidden_state.reshape(x_next.shape), new_up[0], new_down[0], new_up[1], new_down[1], new_up[2], new_down[2])

    return jax.shard_map(local_step, mesh=mesh, in_specs=(rows_spec, P("fsdp"), P("fsdp"), P(), P(), rows_spec, rows_spec, rows_spec, rows_spec, rows_spec, rows_spec, rows_spec, rows_spec), out_specs=(P("fsdp"), rows_spec, rows_spec, rows_spec, rows_spec, rows_spec, rows_spec), check_vma=False)
```

profile of v0, /device:TPU:0, one launch (start us, length us, event | category | flops | bytes accessed | tf_op | source)
XLA Modules:
  0.0 1735.2 jit_solution(9838311268604298901)
XLA Ops:
  7.2 0.0 copy-start.1
  7.2 27.6 %fusion.55 = f32[1536,5120]{1,0:T(8,128)} fusion(bf16[2,1280,5120]{2,1,0:T(8,128)(2,1)} %param.16, bf16[2,1,1536,1280]{3,2,1,0:T(8,128)(2,1)} %param.13), kind=kOutput, calls=%fused_computation.59 | convolution fusion | flops 20132659200 | bytes 48496640 | tf_op jit(solution)/shard_map/dot_general | solution.py:43
  34.8 0.0 copy-done.1
  34.8 31.7 %convolution_convert_fusion = bf16[5120,1280]{1,0:T(8,128)(2,1)} fusion(f32[1536,5120]{1,0:T(8,128)} %fusion.55, bf16[1,1536,1280]{2,1,0:T(8,128)(2,1)S(1)} %copy-done.1), kind=kOutput, calls=%fused_computation.42 | convolution fusion | flops 20209991680 | bytes 48496640 | tf_op jit(solution)/shard_map/dot_general | solution.py:47
  66.5 7.6 all-to-all-start.3
  74.2 44.7 %fusion.6 = bf16[1536,5120]{1,0:T(8,128)(2,1)} fusion(f32[1536,5120]{1,0:T(8,128)} %fusion.55, bf16[2,5120,1280]{2,1,0:T(8,128)(2,1)} %param.17, bf16[1,1536,1280]{2,1,0:T(8,128)(2,1)} %param.14), kind=kOutput, calls=%fused_computation.12 | convolution fusion | flops 20289945600 | bytes 64225280 | tf_op jit(solution)/shard_map/dot_general | solution.py:45
  118.9 26.3 %convolution_convert_fusion.2 = bf16[5120,1280]{0,1:T(8,128)(2,1)} fusion(bf16[1536,5120]{1,0:T(8,128)(2,1)} %fusion.6, bf16[2,1,1536,1280]{3,2,1,0:T(8,128)(2,1)} %param.13), kind=kOutput, calls=%fused_computation.44 | convolution fusion | flops 20139212800 | bytes 32768000 | tf_op jit(solution)/shard_map/dot_general | solution.py:48
  145.2 219.2 %all-to-all-done.3 = bf16[32,160,1280]{2,1,0:T(8,128)(2,1)} async-done(((bf16[32,160,1280]{2,1,0:T(8,128)(2,1)}), bf16[32,160,1280]{2,1,0:T(8,128)(2,1)}, u32[]{:S(2)}, u32[]{:S(2)}) %all-to-all-start.3) | async-done | bytes 13107232 | tf_op jit(solution)/shard_map/all_to_all | solution.py:30
  364.3 4.2 all-to-all-start.1
  368.6 28.3 %fusion.94 = bf16[1536,1280]{1,0:T(8,128)(2,1)} fusion(bf16[1536,5120]{1,0:T(8,128)(2,1)} %fusion.6, bf16[2,1280,5120]{2,1,0:T(8,128)(2,1)} %param.16, bf16[1,1536,1280]{2,1,0:T(8,128)(2,1)} %param.14), kind=kOutput, calls=%fused_computation.73 | convolution fusion | flops 20138557440 | bytes 36700160 | tf_op jit(solution)/shard_map/dot_general | solution.py:50
  396.9 27.6 %fusion.45 = f32[1536,5120]{1,0:T(8,128)} fusion(bf16[2,1280,5120]{2,1,0:T(8,128)(2,1)} %param.16, bf16[2,1,1536,1280]{3,2,1,0:T(8,128)(2,1)} %param.13), kind=kOutput, calls=%fused_computation.53 | convolution fusion | flops 20132659200 | bytes 48496640 | tf_op jit(solution)/shard_map/dot_general | solution.py:43
  424.5 0.0 copy-done.2
  424.5 31.9 %convolution_convert_fusion.1 = bf16[5120,1280]{1,0:T(8,128)(2,1)} fusion(bf16[1536,1280]{1,0:T(8,128)(2,1)S(1)} %copy-done.2, f32[1536,5120]{1,0:T(8,128)} %fusion.45), kind=kOutput, calls=%fused_computation.43 | convolution fusion | flops 20209991680 | bytes 48496640 | tf_op jit(solution)/shard_map/dot_general | solution.py:47
  456.4 202.6 %all-to-all-done.1 = bf16[32,40,5120]{2,1,0:T(8,128)(2,1)} async-done(((bf16[32,40,5120]{2,1,0:T(8,128)(2,1)}), bf16[32,40,5120]{2,1,0:T(8,128)(2,1)}, u32[]{:S(2)}, u32[]{:S(2)}) %all-to-all-start.1) | async-done | bytes 13107232 | tf_op jit(solution)/shard_map/all_to_all | solution.py:30
  659.0 4.0 all-to-all-start.2
  663.0 44.8 %fusion.177 = bf16[1536,5120]{1,0:T(8,128)(2,1)} fusion(f32[1536,5120]{1,0:T(8,128)} %fusion.45, bf16[1536,1280]{1,0:T(8,128)(2,1)} %fusion.94, bf16[2,5120,1280]{2,1,0:T(8,128)(2,1)} %param.17), kind=kOutput, calls=%fused_computation.19.clone.clone.2 | convolution fusion | flops 20289945600 | bytes 64225280 | tf_op jit(solution)/shard_map/dot_general | solution.py:45
  707.8 26.6 %convolution_convert_fusion.3 = bf16[5120,1280]{0,1:T(8,128)(2,1)} fusion(bf16[2,1,1536,1280]{3,2,1,0:T(8,128)(2,1)} %param.13, bf16[1536,5120]{1,0:T(8,128)(2,1)} %fusion.177), kind=kOutput, calls=%fused_computation.45 | convolution fusion | flops 20139212800 | bytes 32768000 | tf_op jit(solution)/shard_map/dot_general | solution.py:48
  734.4 219.0 %all-to-all-done.2 = bf16[32,160,1280]{2,1,0:T(8,128)(2,1)} async-done(((bf16[32,160,1280]{2,1,0:T(8,128)(2,1)}), bf16[32,160,1280]{2,1,0:T(8,128)(2,1)}, u32[]{:S(2)}, u32[]{:S(2)}) %all-to-all-start.2) | async-done | bytes 13107232 | tf_op jit(solution)/shard_map/all_to_all | solution.py:30
  953.3 3.8 all-to-all-start
  957.2 0.0 copy-start
  957.2 0.5 all-gather.9.cloned.1.call-start
  957.7 6.8 convert_reduce_fusion
  964.5 6.8 convert_reduce_fusion.1
  971.4 1.0 multiply_reduce_fusion
  972.4 7.5 convert_reduce_fusion.2
  980.0 267.7 %all-to-all-done = bf16[32,40,5120]{2,1,0:T(8,128)(2,1)} async-done(((bf16[32,40,5120]{2,1,0:T(8,128)(2,1)}), bf16[32,40,5120]{2,1,0:T(8,128)(2,1)}, u32[]{:S(2)}, u32[]{:S(2)}) %all-to-all-start) | async-done | bytes 13107232 | tf_op jit(solution)/shard_map/all_to_all | solution.py:30
  1247.6 7.5 convert_reduce_fusion.3
  1255.2 2.5 multiply_reduce_fusion.1
  1258.9 37.0 %psum.7 = f32[]{:T(128)} all-reduce(f32[]{:T(128)S(6)} %add.83), channel_id=1, replica_groups=mesh['fsdp'=32] {'fsdp'}, use_global_device_ids=true, to_apply=%region_6.0 | all-reduce | flops 1 | bytes 8 | tf_op jit(solution)/shard_map/psum | solution.py:56
  1296.6 6.1 fusion.140
  1302.8 1.0 fusion.144
  1303.7 0.0 all-gather.9.cloned.1.call-update
  1303.7 0.0 all-gather.11.cloned.1.call-start
  1303.8 6.0 fusion.142
  1309.8 1.0 fusion.145
  1310.8 0.0 all-gather.11.cloned.1.call-update
  1310.8 0.0 all-gather.13.cloned.1.call-start
  1310.8 0.7 all-gather.13.cloned.1.call-update
  1311.5 0.0 all-gather.15.cloned.1.call-start
  1311.6 0.5 all-gather.15.cloned.1.call-update
  1312.1 90.1 %all-gather.9.cloned.1.call-done = bf16[1,1280,5120]{2,1,0:T(8,128)(2,1)} async-done(((bf16[1,40,5120]{2,1,0:T(8,128)(2,1)}), bf16[1,1280,5120]{2,1,0:T(8,128)(2,1)}) %all-gather.9.cloned.1.call-update) | async-done | bytes 13107216 | tf_op jit(solution)/shard_map/all_gather | solution.py:72
  1402.2 34.3 %fusion.21.clone.8 = bf16[1536,5120]{1,0:T(8,128)(2,1)} fusion(bf16[1,1280,5120]{2,1,0:T(8,128)(2,1)} %all-gather.9.cloned.1.call-done, bf16[1,1536,1280]{2,1,0:T(8,128)(2,1)} %param.15), kind=kOutput, calls=%fused_computation.27.clone.clone.clone.clone.clone.clone.clone.1 | convolution fusion | flops 20203438080 | bytes 32768000 | tf_op jit(solution)/shard_map/dot_general | solution.py:74
  1436.5 65.5 %all-gather.11.cloned.1.call-done = bf16[1,5120,1280]{2,1,0:T(8,128)(2,1)} async-done(((bf16[1,160,1280]{2,1,0:T(8,128)(2,1)}), bf16[1,5120,1280]{2,1,0:T(8,128)(2,1)}) %all-gather.11.cloned.1.call-update) | async-done | bytes 13107216 | tf_op jit(solution)/shard_map/all_gather | solution.py:73
  1501.9 28.1 %fusion.89 = bf16[1536,1280]{1,0:T(8,128)(2,1)} fusion(bf16[1,5120,1280]{2,1,0:T(8,128)(2,1)} %all-gather.11.cloned.1.call-done, bf16[1,1536,1280]{2,1,0:T(8,128)(2,1)} %param.15, bf16[1536,5120]{1,0:T(8,128)(2,1)} %fusion.21.clone.8), kind=kOutput, calls=%fused_computation.72 | convolution fusion | flops 20138557440 | bytes 36700160 | tf_op jit(solution)/shard_map/dot_general | solution.py:76
  1530.1 71.0 %all-gather.13.cloned.1.call-done = bf16[1,1280,5120]{2,1,0:T(8,128)(2,1)} async-done(((bf16[1,40,5120]{2,1,0:T(8,128)(2,1)}), bf16[1,1280,5120]{2,1,0:T(8,128)(2,1)}) %all-gather.13.cloned.1.call-update) | async-done | bytes 13107216 | tf_op jit(solution)/shard_map/all_gather | solution.py:72
  1601.1 34.5 %fusion.184 = bf16[1536,5120]{1,0:T(8,128)(2,1)} fusion(bf16[1536,1280]{1,0:T(8,128)(2,1)} %fusion.89, bf16[1,1280,5120]{2,1,0:T(8,128)(2,1)} %all-gather.13.cloned.1.call-done), kind=kOutput, calls=%fused_computation.35.clone.clone.clone.clone.clone.clone.clone.clone.1 | convolution fusion | flops 20203438080 | bytes 32768000 | tf_op jit(solution)/shard_map/dot_general | solution.py:74
  1635.5 64.6 %all-gather.15.cloned.1.call-done = bf16[1,5120,1280]{2,1,0:T(8,128)(2,1)} async-done(((bf16[1,160,1280]{2,1,0:T(8,128)(2,1)}), bf16[1,5120,1280]{2,1,0:T(8,128)(2,1)}) %all-gather.15.cloned.1.call-update) | async-done | bytes 13107216 | tf_op jit(solution)/shard_map/all_gather | solution.py:73
  1700.1 28.1 %fusion.97 = bf16[1,1536,1280]{2,1,0:T(8,128)(2,1)} fusion(bf16[1,5120,1280]{2,1,0:T(8,128)(2,1)} %all-gather.15.cloned.1.call-done, bf16[1536,1280]{1,0:T(8,128)(2,1)} %fusion.89, bf16[1536,5120]{1,0:T(8,128)(2,1)} %fusion.184), kind=kOutput, calls=%fused_computation.74 | convolution fusion | flops 20138557440 | bytes 36700160 | tf_op jit(solution)/shard_map/dot_general | solution.py:76
  (2 shorter events, 0.0 us)
Async XLA Ops:
  7.2 27.6 %copy-start.1 = (bf16[1,1536,1280]{2,1,0:T(8,128)(2,1)S(1)}, bf16[1,1536,1280]{2,1,0:T(8,128)(2,1)}, u32[]{:S(2)}) copy-start(bf16[1,1536,1280]{2,1,0:T(8,128)(2,1)} %param.14) | copy-start | bytes 11796484
  66.5 297.8 %all-to-all-start.3 = ((bf16[32,160,1280]{2,1,0:T(8,128)(2,1)}), bf16[32,160,1280]{2,1,0:T(8,128)(2,1)}, u32[]{:S(2)}, u32[]{:S(2)}) async-start(bf16[32,160,1280]{2,1,0:T(8,128)(2,1)} %bitcast.144), calls=%async_computation.3 | async-start | bytes 26214400 | tf_op jit(solution)/shard_map/all_to_all | solution.py:30
  364.3 294.6 %all-to-all-start.1 = ((bf16[32,40,5120]{2,1,0:T(8,128)(2,1)}), bf16[32,40,5120]{2,1,0:T(8,128)(2,1)}, u32[]{:S(2)}, u32[]{:S(2)}) async-start(bf16[32,40,5120]{2,1,0:T(8,128)(2,1)} %bitcast.143), calls=%async_computation.1 | async-start | bytes 26214400 | tf_op jit(solution)/shard_map/all_to_all | solution.py:30
  396.9 27.6 %copy-start.2 = (bf16[1536,1280]{1,0:T(8,128)(2,1)S(1)}, bf16[1536,1280]{1,0:T(8,128)(2,1)}, u32[]{:S(2)}) copy-start(bf16[1536,1280]{1,0:T(8,128)(2,1)} %fusion.94) | copy-start | bytes 11796484
  659.0 294.4 %all-to-all-start.2 = ((bf16[32,160,1280]{2,1,0:T(8,128)(2,1)}), bf16[32,160,1280]{2,1,0:T(8,128)(2,1)}, u32[]{:S(2)}, u32[]{:S(2)}) async-start(bf16[32,160,1280]{2,1,0:T(8,128)(2,1)} %bitcast.142), calls=%async_computation.2 | async-start | bytes 26214400 | tf_op jit(solution)/shard_map/all_to_all | solution.py:30
  953.3 294.3 %all-to-all-start = ((bf16[32,40,5120]{2,1,0:T(8,128)(2,1)}), bf16[32,40,5120]{2,1,0:T(8,128)(2,1)}, u32[]{:S(2)}, u32[]{:S(2)}) async-start(bf16[32,40,5120]{2,1,0:T(8,128)(2,1)} %bitcast.141), calls=%async_computation | async-start | bytes 26214400 | tf_op jit(solution)/shard_map/all_to_all | solution.py:30
  957.2 14.2 copy-start
  957.2 445.0 %all-gather.9.cloned.1.call-start = ((), (), s32[]{:S(2)}) async-start(), calls=%async_computation.4 | async-start | bytes 13516800 | tf_op jit(solution)/shard_map/all_gather | solution.py:72
  1303.7 198.2 %all-gather.11.cloned.1.call-start = ((), (), s32[]{:S(2)}) async-start(), calls=%async_computation.5 | async-start | bytes 13516800 | tf_op jit(solution)/shard_map/all_gather | solution.py:73
  1310.8 290.3 %all-gather.13.cloned.1.call-start = ((), (), s32[]{:S(2)}) async-start(), calls=%async_computation.6 | async-start | bytes 13516800 | tf_op jit(solution)/shard_map/all_gather | solution.py:72
  1311.5 388.6 %all-gather.15.cloned.1.call-start = ((), (), s32[]{:S(2)}) async-start(), calls=%async_computation.7 | async-start | bytes 13516800 | tf_op jit(solution)/shard_map/all_gather | solution.py:73
Sparse Core Ops, SparseCore 0:
  1303.8 98.2 all-gather.8
  1405.6 96.2 all-gather.10
  1504.8 96.2 all-gather.12
  1603.8 96.3 all-gather.14
where the time goes:
time: 1740 us
  waiting for transfers between devices  1200 us (69%)
  matrix products  415 us (24%)
  other arithmetic  44.4 us (3%)
  blocking collectives  37 us (2%)
  starting transfers between devices  20.3 us (1%)
    all_to_all x4, waiting for transfers between devices, reduce_rows(): received = lax.all_to_all(part_grad, 'fsdp', 0, 0, tiled=True)  908 us
    all_gather x2, waiting for transfers between devices, local_step(): w_layer_up = lax.all_gather(up_shard[layer_idx], 'fsdp', axis=0, tiled=True)  161 us
    all_gather x2, waiting for transfers between devices, local_step(): lax.all_gather(down_shard[layer_idx], 'fsdp', axis=0, tiled=True)  130 us
    dot_general x2, matrix products, backward_update(): lax.dot_general(grad_cur, w_down[layer_idx], (((1,), (1,)), ((), ())), pr...  89.5 us
    dot_general x2, matrix products, local_step(): jnp.dot(hidden_state, w_layer_up, preferred_element_type=jnp.float32)  68.8 us
    dot_general x2, matrix products, backward_update(): lax.dot_general(hidden_act.astype(jnp.bfloat16), grad_cur, (((0,), (0,)),...  63.6 us
    dot_general x2, matrix products, local_step(): jnp.dot(hidden_act, w_layer_down, preferred_element_type=jnp.float32)  56.3 us
    dot_general x2, matrix products, backward_update(): pre_act = jnp.dot(x_in, w_up[layer_idx], preferred_element_type=jnp.float32)  55.3 us
  transfers between devices with their start and end apart: 8, of which 8 were waited for; matrix products, arithmetic and copies ran while one was open for 21% of the time, Pallas kernels for 0%

commit v1 on v0

v1 whole, which is shorter than its diff:
```python
import functools
import math
import jax
import jax.numpy as jnp
from jax import lax
from jax.experimental import pallas as pl
from jax.experimental.pallas import tpu as pltpu
from jax.sharding import PartitionSpec as P


LEARN_RATE = 0.001
BETA_ONE = 0.9
BETA_TWO = 0.95
ADAM_EPS = 1e-8
WEIGHT_DECAY = 0.1
ADAM_STEP = 3
MICRO_STEPS = 2
GELU_SCALE = math.sqrt(2.0 / math.pi)
GELU_CUBIC = 0.044715


F32 = jnp.float32
BF16 = jnp.bfloat16
MASKS = {"z": 8, "y": 4, "x": 2, "c": 1}
SIZES = {"z": 4, "y": 2, "x": 2, "c": 2}


def gelu_fn(pre_act):
    return jax.nn.gelu(pre_act, approximate=True)


def adamw_update(master_old, mom_one, mom_two, grad_clip):
    mom_one_new = BETA_ONE * mom_one + (1.0 - BETA_ONE) * grad_clip
    mom_two_new = BETA_TWO * mom_two + (1.0 - BETA_TWO) * grad_clip * grad_clip
    first_hat = mom_one_new / (1.0 - BETA_ONE ** ADAM_STEP)
    second_hat = mom_two_new / (1.0 - BETA_TWO ** ADAM_STEP)
    master_new = master_old - LEARN_RATE * (first_hat / (jnp.sqrt(second_hat) + ADAM_EPS) + WEIGHT_DECAY * master_old)
    return master_new, mom_one_new, mom_two_new


def dot(lhs, rhs, lhs_dim, rhs_dim):
    return lax.dot_general(lhs, rhs, (((lhs_dim,), (rhs_dim,)), ((), ())), preferred_element_type=F32)


def pick(value, axis, index):
    return lax.dynamic_index_in_dim(value, index, axis, keepdims=False)


class Chain:
    def __init__(self):
        self.last = None
        self.index = 0

    def step(self, compute, values, wait=None):
        self.index += 1
        if self.last is not None:
            values, _ = lax.optimization_barrier((values, self.last))
        result = compute(values)
        self.last = result if wait is None else wait(result)
        return result


class Place:
    def __init__(self, n_dev, chain):
        dev = lax.axis_index("fsdp")
        self.n_dev = n_dev
        self.chain = chain
        self.at = {"c": dev & 1, "x": (dev >> 1) & 1, "y": (dev >> 2) & 1, "z": dev >> 3}

    def swap(self, value, mask):
        return lax.ppermute(value, "fsdp", [(i, i ^ mask) for i in range(self.n_dev)])


class Reduce:
    def __init__(self, place, part, rows, order, cols=None, depth=4):
        self.place, self.order = place, order
        self.dims = ["z", "y", "x"]
        self.rows, self.depth = rows, depth
        self.cols = cols or (0, part.shape[1])
        self.part = part.reshape(depth, 2, 2, 2, rows, part.shape[1])

    def block(self, part, dim, flip, flip_core):
        sizes = [self.depth, 2, 2, 1, self.rows, self.cols[1] - self.cols[0]]
        starts = [0, 0, 0, self.place.at["c"] ^ flip_core, 0, self.cols[0]]
        axis = self.dims.index(dim)
        sizes[axis] = 1
        starts[axis] = self.place.at[dim] ^ flip
        piece = lax.dynamic_slice(part, starts, sizes)
        return piece.reshape([n for i, n in enumerate(sizes) if i not in (3, axis)])

    def first(self):
        dim = self.order[0]
        flips = [(flip, core) for flip in range(SIZES[dim]) for core in (0, 1)]
        pieces = self.place.chain.step(lambda part: [self.block(part, dim, *flip) for flip in flips[1:]], self.part)
        self.terms = [self.block(self.part, dim, 0, 0)]
        for (flip, core), piece in zip(flips[1:], pieces):
            self.terms.append(self.place.swap(piece, flip * MASKS[dim] + core))
        self.dims.remove(dim)
        self.stage = 1

    def total(self, terms, axis, index):
        picked = [pick(term, axis, index).astype(F32) for term in terms]
        while len(picked) > 1:
            picked = [sum(picked[i:i + 2]) for i in range(0, len(picked), 2)]
        return picked[0]

    def next(self):
        dim = self.order[self.stage]
        axis = self.dims.index(dim)
        mine = self.place.at[dim]
        flips = range(1, SIZES[dim])
        sends = self.place.chain.step(lambda terms: [self.total(terms, axis, mine ^ flip) for flip in flips], self.terms)
        self.terms = [pick(term, axis, mine) for term in self.terms]
        self.terms += [self.place.swap(send, flip * MASKS[dim]) for flip, send in zip(flips, sends)]
        self.dims.remove(dim)
        self.stage += 1

    def sum(self, terms):
        return self.total([term[None] for term in terms], 0, 0)


class ReduceSplit:
    def __init__(self, place, low, high):
        self.place, self.low, self.high = place, low, high

    def merge(self):
        def both(terms):
            whole = jnp.concatenate([self.low.sum(terms[0]), self.high.sum(terms[1])], axis=0)
            return [pick(whole, 0, self.place.at["z"] ^ flip) for flip in range(4)]

        sends = self.place.chain.step(both, (self.low.terms, self.high.terms))
        self.terms = [sends[0]] + [self.place.swap(sends[flip], 8 * flip) for flip in (1, 2, 3)]

    def sum(self, terms):
        return sum(terms)


def join_kernel(last, where, own, far, own_core, far_core, *refs):
    out = refs[-1]
    core = where[3]
    bit = where[{"y": 1, "x": 2}[last]]
    for ref, flip, flip_core in ((own, 0, 0), (far, 1, 0), (own_core, 0, 1), (far_core, 1, 1)):
        if last == "x":
            out[0, 0, bit ^ flip, core ^ flip_core] = ref[0, 0]
        else:
            out[0, bit ^ flip, 0, core ^ flip_core] = ref[0, 0]


def join(last, where, pieces, whole, cols, half):
    rows, part = pieces[0].shape[2:]

    def in_map(i, j, where):
        return (i, j, 0, 0)

    def out_map(i, j, where):
        if last == "x":
            return (where[0] ^ j, where[1] ^ i, 0, 0, 0, half)
        return (where[0] ^ j, 0, where[2] ^ i, 0, 0, half)

    block = (1, 1, 2, 2, rows, part) if last == "x" else (1, 2, 1, 2, rows, part)
    in_specs = [pl.BlockSpec((1, 1, rows, part), in_map)] * 4
    args = list(pieces)
    aliases = {}
    if whole is not None:
        in_specs = in_specs + [pl.BlockSpec(memory_space=pl.ANY)]
        args.append(whole)
        aliases = {5: 0}
    return pl.pallas_call(
        functools.partial(join_kernel, last),
        grid_spec=pltpu.PrefetchScalarGridSpec(num_scalar_prefetch=1, grid=(2, 4), in_specs=in_specs, out_specs=pl.BlockSpec(block, out_map)),
        out_shape=jax.ShapeDtypeStruct((4, 2, 2, 2, rows, cols), BF16),
        input_output_aliases=aliases,
        cost_estimate=pl.CostEstimate(flops=10 ** 9, bytes_accessed=8 * 8 * rows * part * 2, transcendentals=0),
    )(where, *args)


class Gather:
    def __init__(self, place, where, shard):
        self.place, self.where, self.cols = place, where, shard.shape[1]
        self.shard = shard
        self.second = ["y", "x"]
        self.third = ["x", "y"]

    def send_z(self):
        half = self.cols // 2
        pieces = self.place.chain.step(lambda shard: [shard[:, :half], shard[:, half:]], self.shard)
        self.pieces = [[piece] + [self.place.swap(piece, 8 * flip) for flip in (1, 2, 3)] for piece in pieces]

    def send_second(self):
        stacks = self.place.chain.step(lambda pieces: [jnp.stack(piece) for piece in pieces], self.pieces)
        self.pieces = [[stack, self.place.swap(stack, MASKS[dim])] for stack, dim in zip(stacks, self.second)]

    def send_third(self):
        stacks = self.place.chain.step(lambda pieces: [jnp.stack(piece) for piece in pieces], self.pieces)
        self.pieces = [[stack, self.place.swap(stack, MASKS[dim]), self.place.swap(stack, 1)] for stack, dim in zip(stacks, self.third)]

    def send_core(self):
        far = self.place.chain.step(lambda value: value, [piece[1] for piece in self.pieces])
        self.pieces = [[piece[0], got, piece[2], self.place.swap(got, 1)] for piece, got in zip(self.pieces, far)]

    def whole(self):
        def both(pieces):
            left = join("x", self.where, pieces[0], None, self.cols, 0)
            return join("y", self.where, pieces[1], left, self.cols, 1).reshape(-1, self.cols)

        return self.place.chain.step(both, self.pieces)


def hidden_kernel(n_split, x_ref, g_ref, up_ref, down_ref, *refs):
    act_ref, pre_ref = refs[-2:]
    step = x_ref.shape[0] // n_split
    for i in range(n_split):
        rows = pl.ds(i * step, step)
        h = dot(x_ref[rows, :], up_ref[...], 1, 0)
        d_act = dot(g_ref[rows, :], down_ref[...], 1, 1)
        square = h * h
        t = jnp.tanh(GELU_SCALE * h * (1.0 + GELU_CUBIC * square))
        half = 0.5 * (1.0 + t)
        slope = half + 0.5 * h * (1.0 - t * t) * (GELU_SCALE * (1.0 + 3.0 * GELU_CUBIC * square))
        act_ref[rows, :] = (h * half).astype(BF16)
        pre_ref[rows, :] = (d_act * slope).astype(BF16)


def hidden_pair(layer, x_tokens, grad_cur, w_up, w_down, part=0, n_parts=1, slopes=None):
    _, tokens, width = x_tokens.shape
    ff_width = w_up.shape[2]
    tile = 512
    steps = ff_width // tile // n_parts
    base = part * steps
    kernel = functools.partial(hidden_kernel, 6)
    in_specs = [
        pl.BlockSpec((None, tokens, width), lambda j: (layer, 0, 0)),
        pl.BlockSpec((tokens, width), lambda j: (0, 0)),
        pl.BlockSpec((None, width, tile), lambda j: (layer, 0, base + j)),
        pl.BlockSpec((None, tile, width), lambda j: (layer, base + j, 0)),
    ]
    args = [x_tokens, grad_cur, w_up, w_down]
    aliases = {}
    if slopes is not None:
        in_specs.append(pl.BlockSpec(memory_space=pl.ANY))
        args.append(slopes)
        aliases = {4: 1}
    return pl.pallas_call(
        kernel,
        grid=(steps,),
        in_specs=in_specs,
        out_specs=[pl.BlockSpec((tokens, tile), lambda j: (0, j)), pl.BlockSpec((tokens, tile), lambda j: (0, base + j))],
        out_shape=(jax.ShapeDtypeStruct((tokens, ff_width // n_parts), BF16), jax.ShapeDtypeStruct((tokens, ff_width), BF16)),
        input_output_aliases=aliases,
        compiler_params=pltpu.CompilerParams(vmem_limit_bytes=56 * 2 ** 20),
        cost_estimate=pl.CostEstimate(flops=4 * tokens * width * ff_width // n_parts, bytes_accessed=70 * 10 ** 6 // n_parts, transcendentals=tokens * ff_width // n_parts),
    )(*args)


def total_square(value, place):
    value = value.reshape(1, 1)
    value = value + place.swap(value, 1) + place.swap(value, 2) + place.swap(value, 3)
    value = value + place.swap(value, 4) + place.swap(value, 8) + place.swap(value, 12)
    return (value + place.swap(value, 16))[0, 0]


def solution(mesh):
    n_dev = mesh.shape["fsdp"]
    rows_spec = P(None, "fsdp")

    def run(x_saved, grad_out, x_next, w_up, w_down, gacc_up, gacc_down, master_up, master_down, mom1_up, mom1_down, mom2_up, mom2_down):
        chain = Chain()
        place = Place(n_dev, chain)
        layers, model_width, ff_width = w_up.shape
        clip_norm = 0.1 * math.sqrt(2 * layers * model_width * ff_width)
        x_tokens = x_saved.reshape(layers, -1, model_width)
        grad_two = grad_out.reshape(-1, model_width)
        rows_up, rows_down = gacc_up.shape[1], gacc_down.shape[1]

        def weight_grad(pair):
            return dot(pair[0], pair[1], 0, 0).astype(BF16)

        def split(part, rows, *orders):
            cols = part.shape[1] // len(orders)
            return [Reduce(place, part, rows, order, (i * cols, (i + 1) * cols)) for i, order in enumerate(orders)]

        act_low, slopes = chain.step(lambda v: hidden_pair(1, *v, part=0, n_parts=2), (x_tokens, grad_two, w_up, w_down))
        down_low = Reduce(place, chain.step(weight_grad, (act_low, grad_two)), rows_down, "xy", depth=2)
        down_low.first()
        act_high, pre_two = chain.step(lambda v: hidden_pair(1, *v[:4], part=1, n_parts=2, slopes=v[4]), (x_tokens, grad_two, w_up, w_down, slopes))
        down_high = Reduce(place, chain.step(weight_grad, (act_high, grad_two)), rows_down, "yx", depth=2)
        down_high.first()
        down_two = ReduceSplit(place, down_low, down_high)
        up_two = split(chain.step(weight_grad, (x_tokens[1], pre_two)), rows_up, "xyz", "yxz")
        for chunk in up_two:
            chunk.first()
        grad_one = chain.step(lambda v: (v[1].astype(F32) + dot(v[0], v[2], 1, 1)).astype(BF16), (pre_two, grad_two, w_up[1]))
        down_low.next()
        act_one, pre_one = chain.step(lambda v: hidden_pair(0, *v), (x_tokens, grad_one, w_up, w_down))
        down_high.next()
        down_one = split(chain.step(weight_grad, (act_one, grad_one)), rows_down, "xyz", "yxz")
        for chunk in down_one:
            chunk.first()
        for chunk in up_two:
            chunk.next()
        up_one = split(chain.step(weight_grad, (x_tokens[0], pre_one)), rows_up, "xyz", "yxz", "xyz", "yxz")
        down_two.merge()
        up_one[0].first()
        up_one[1].first()
        for chunk in up_two:
            chunk.next()
        for chunk in down_one:
            chunk.next()
        up_one[2].first()
        up_one[3].first()
        up_one[0].next()
        up_one[1].next()
        for chunk in down_one:
            chunk.next()
        up_one[2].next()
        up_one[3].next()

        def grads_of(chunks):
            def add(values):
                terms, gacc = values
                sums = [chunk.sum(term) for chunk, term in zip(chunks, terms)]
                return (gacc + (sums[0] if len(sums) == 1 else jnp.concatenate(sums, axis=1))) / MICRO_STEPS

            return add

        def finish(chunks, gacc):
            return chain.step(grads_of(chunks), ([chunk.terms for chunk in chunks], gacc))

        up_one[0].next()
        up_one[1].next()
        grad_down_two = finish([down_two], gacc_down[1])
        grad_up_two = finish(up_two, gacc_up[1])
        grad_down_one = finish(down_one, gacc_down[0])
        up_one[2].next()
        up_one[3].next()
        grad_up_one = finish(up_one, gacc_up[0])

        grads = (grad_up_one, grad_down_one, grad_up_two, grad_down_two)
        local_sq = chain.step(lambda v: sum(jnp.sum(g * g) for g in v), grads)
        clip_factor = jnp.minimum(1.0, clip_norm / jnp.sqrt(total_square(local_sq, place)))
        chain.last = None
        new_up = chain.step(lambda v: adamw_update(*v[:3], jnp.stack(v[3:5]) * v[5]), (master_up, mom1_up, mom2_up, grad_up_one, grad_up_two, clip_factor))
        where = jnp.stack([place.at[d] for d in "zyxc"]).astype(jnp.int32)
        up_a, up_b = [Gather(place, where, new_up[0][i].astype(BF16)) for i in (0, 1)]
        up_a.send_z()
        new_down = chain.step(lambda v: adamw_update(*v[:3], jnp.stack(v[3:5]) * v[5]), (master_down, mom1_down, mom2_down, grad_down_one, grad_down_two, clip_factor))
        down_a, down_b = [Gather(place, where, new_down[0][i].astype(BF16)) for i in (0, 1)]
        down_a.send_z()
        up_b.send_z()
        up_a.send_second()
        down_b.send_z()
        up_a.send_third()
        down_a.send_second()
        up_a.send_core()
        down_a.send_third()
        up_b.send_second()

        def up_mul(values):
            return gelu_fn(dot(values[0], values[1], 1, 0)).astype(BF16)

        def down_mul(values):
            return (values[0].astype(F32) + dot(values[1], values[2], 1, 0)).astype(BF16)

        hidden_state = x_next.reshape(-1, model_width)
        act = chain.step(up_mul, (hidden_state, up_a.whole()))
        down_a.send_core()
        up_b.send_third()
        down_b.send_second()
        hidden_state = chain.step(down_mul, (hidden_state, act, down_a.whole()))
        up_b.send_core()
        down_b.send_third()
        act = chain.step(up_mul, (hidden_state, up_b.whole()))
        down_b.send_core()
        hidden_state = chain.step(down_mul, (hidden_state, act, down_b.whole()))
        return (hidden_state.reshape(x_next.shape), new_up[0], new_down[0], new_up[1], new_down[1], new_up[2], new_down[2])

    return jax.shard_map(run, mesh=mesh, in_specs=(rows_spec, P("fsdp"), P("fsdp"), P(), P(), rows_spec, rows_spec, rows_spec, rows_spec, rows_spec, rows_spec, rows_spec, rows_spec), out_specs=(P("fsdp"), rows_spec, rows_spec, rows_spec, rows_spec, rows_spec, rows_spec), check_vma=False)
```

time: 1740 us -> 1370 us (0.79)
  waiting for transfers between devices: 1200 us -> 490 us
  starting transfers between devices: 20.3 us -> 245 us
  Pallas kernels: 0 us -> 187 us
  matrix products: 415 us -> 256 us
  local copies, waits for them, and re-layouts: 1.92 us -> 114 us
  blocking collectives: 37 us -> 0 us
    all_to_all x4 -> x0, waiting for transfers between devices: 908 us -> none  [reduce_rows(): received = lax.all_to_all(part_grad, 'fsdp', 0, 0, tiled=True)]
    ppermute x0 -> x130, waiting for transfers between devices: none -> 490 us  [swap(): lax.ppermute(value, 'fsdp', [(i, i ^ mask) for i in range(self.n_dev)])]
    all_gather x4 -> x0, waiting for transfers between devices: 291 us -> none  [the longest x2 161 us: local_step(): w_layer_up = lax.all_gather(up_shard[layer_idx], 'fsdp', axis=0, tiled=True)]
    ppermute x0 -> x130, starting transfers between devices: none -> 245 us  [swap(): lax.ppermute(value, 'fsdp', [(i, i ^ mask) for i in range(self.n_dev)])]
    pallas_call x0 -> x11, Pallas kernels: none -> 187 us  [the longest x3 116 us: hidden_pair(): pl.pallas_call(kernel, grid=(steps,), in_specs=in_specs, out_specs=[pl.Bl...]
    dot_general x13 -> x10, matrix products: 415 us -> 256 us  [dot(): lax.dot_general(lhs, rhs, (((lhs_dim,), (rhs_dim,)), ((), ())), preferred...]
    squeeze x0 -> x73, local copies, waits for them, and re-layouts: none -> 49.7 us  [the longest x69 27.8 us: pick(): return lax.dynamic_index_in_dim(value, index, axis, keepdims=False)]
    psum x1 -> x0, blocking collectives: 37 us -> none  [backward_update(): lax.psum(local_sq, 'fsdp')]
  transfers between devices with their start and end apart: 8 -> 130, of which waited for: 8 -> 53; matrix products, arithmetic and copies ran while one was open for 21% -> 26% of each run, Pallas kernels for 0% -> 10%
where the time goes in v1:
time: 1370 us; the launch traced here: 1360 us
  waiting for transfers between devices  490 us (36%)
  matrix products  256 us (19%)
  starting transfers between devices  245 us (18%)
  Pallas kernels  187 us (14%)
  local copies, waits for them, and re-layouts  114 us (8%)
  other arithmetic  53.5 us (4%)
    ppermute x130, waiting for transfers between devices, swap(): lax.ppermute(value, 'fsdp', [(i, i ^ mask) for i in range(self.n_dev)])  490 us
    dot_general x10, matrix products, dot(): lax.dot_general(lhs, rhs, (((lhs_dim,), (rhs_dim,)), ((), ())), preferred...  256 us
    ppermute x130, starting transfers between devices, swap(): lax.ppermute(value, 'fsdp', [(i, i ^ mask) for i in range(self.n_dev)])  245 us
    pallas_call x3, Pallas kernels, hidden_pair(): pl.pallas_call(kernel, grid=(steps,), in_specs=in_specs, out_specs=[pl.Bl...  116 us
    pallas_call x8, Pallas kernels, join(): pl.pallas_call(functools.partial(join_kernel, last), grid_spec=pltpu.Pref...  70.4 us
    dynamic_slice x33, local copies, waits for them, and re-layouts, block(): piece = lax.dynamic_slice(part, starts, sizes)  30.4 us
    squeeze x69, local copies, waits for them, and re-layouts, pick(): return lax.dynamic_index_in_dim(value, index, axis, keepdims=False)  27.8 us
  transfers between devices with their start and end apart: 130, of which 53 were waited for; matrix products, arithmetic and copies ran while one was open for 26% of the time, Pallas kernels for 10%

profile of v1, /device:TPU:0, one launch (start us, length us, event | category | flops | bytes accessed | tf_op | source)
XLA Modules:
  0.0 1355.3 jit_solution(4874501356128294668)
XLA Ops:
  0.7 30.3 %shard_map.180 = (bf16[1536,2560]{1,0:T(8,128)(2,1)}, bf16[1536,5120]{1,0:T(8,128)(2,1)}) custom-call(bf16[2,1536,1280]{2,1,0:T(8,128)(2,1)} %bitcast.465, bf16[1536,1280]{1,0:T(8,128)(2,1)} %bitcast.500, bf16[2,1280,5120]{2,1,0:T(8,128)(2,1)} %up_ref.3, bf16[2,5120,1280]{2,1,0:T(8,128)(2,1)} %down_ref.3), custom_call_target="tpu_custom_call" | custom-call | flops 20132659200 | bytes 35000000 | tf_op jit(solution)/shard_map/pallas_call | solution.py:243
  31.0 14.5 %convolution_convert_fusion.4 = bf16[2560,1280]{1,0:T(8,128)(2,1)} fusion(bf16[1536,2560]{1,0:T(8,128)(2,1)} %get-tuple-element.321, bf16[1536,1280]{1,0:T(8,128)(2,1)S(1)} %bitcast.503), kind=kOutput, calls=%fused_computation.23 | convolution fusion | flops 10069606400 | bytes 18350080 | tf_op jit(solution)/shard_map/dot_general | solution.py:42
  55.1 31.2 %shard_map.181 = (bf16[1536,2560]{1,0:T(8,128)(2,1)}, bf16[1536,5120]{1,0:T(8,128)(2,1)}) custom-call(bf16[2,1536,1280]{2,1,0:T(8,128)(2,1)} %bitcast.466, bf16[1536,1280]{1,0:T(8,128)(2,1)} %bitcast.501, bf16[2,1280,5120]{2,1,0:T(8,128)(2,1)} %up_ref.3, bf16[2,5120,1280]{2,1,0:T(8,128)(2,1)} %down_ref.3, ...), custom_call_target="tpu_custom_call", output_to_operand_aliasing={{1}: (4, {})} | custom-call | flops 20132659200 | bytes 35000000 | tf_op jit(solution)/shard_map/pallas_call | solution.py:243
  86.3 14.5 %convolution_convert_fusion.3 = bf16[2560,1280]{1,0:T(8,128)(2,1)} fusion(bf16[1536,2560]{1,0:T(8,128)(2,1)} %get-tuple-element.331, bf16[1536,1280]{1,0:T(8,128)(2,1)S(1)} %bitcast.504), kind=kOutput, calls=%fused_computation.22 | convolution fusion | flops 10069606400 | bytes 18350080 | tf_op jit(solution)/shard_map/dot_general | solution.py:42
  114.7 12.8 slice_bitcast_fusion
  131.7 24.9 %convolution_convert_fusion.1 = bf16[1280,5120]{1,0:T(8,128)(2,1)S(1)} fusion(bf16[1536,1280]{1,0:T(8,128)(2,1)} %get-tuple-element.334, bf16[1536,5120]{1,0:T(8,128)(2,1)S(1)} %bitcast.489), kind=kOutput, calls=%fused_computation.19 | convolution fusion | flops 20139212800 | bytes 32768000 | tf_op jit(solution)/shard_map/dot_general | solution.py:42
  181.1 28.3 %fusion.16.g_ref = bf16[1536,1280]{1,0:T(8,128)(2,1)} fusion(bf16[1536,5120]{1,0:T(8,128)(2,1)} %get-tuple-element.339, bf16[1280,5120]{1,0:T(8,128)(2,1)} %slice_bitcast_fusion, bf16[1536,1280]{1,0:T(8,128)(2,1)} %bitcast.502), kind=kOutput, calls=%fused_computation.27 | convolution fusion | flops 20138557440 | bytes 36700160 | tf_op jit(solution)/shard_map/dot_general | solution.py:42
  220.8 54.8 %shard_map.182 = (bf16[1536,5120]{1,0:T(8,128)(2,1)}, bf16[1536,5120]{1,0:T(8,128)(2,1)}) custom-call(bf16[2,1536,1280]{2,1,0:T(8,128)(2,1)} %bitcast.467, bf16[1536,1280]{1,0:T(8,128)(2,1)} %fusion.16.g_ref, bf16[2,1280,5120]{2,1,0:T(8,128)(2,1)} %up_ref.3, bf16[2,5120,1280]{2,1,0:T(8,128)(2,1)} %down_ref.3), custom_call_target="tpu_custom_call" | custom-call | flops 40265318400 | bytes 70000000 | tf_op jit(solution)/shard_map/pallas_call | solution.py:243
  281.5 25.2 %convolution_convert_fusion.2 = bf16[5120,1280]{1,0:T(8,128)(2,1)S(1)} fusion(bf16[1536,5120]{1,0:T(8,128)(2,1)} %get-tuple-element.355, bf16[1536,1280]{1,0:T(8,128)(2,1)} %fusion.16.g_ref), kind=kOutput, calls=%fused_computation.20 | convolution fusion | flops 20139212800 | bytes 32768000 | tf_op jit(solution)/shard_map/dot_general | solution.py:42
  316.8 32.3 %collective-permute-done.8 = bf16[4,2,40,2560]{3,2,0,1:T(8,128)(2,1)S(1)} collective-permute-done((bf16[4,2,40,2560]{3,2,0,1:T(8,128)(2,1)S(1)}, bf16[4,2,40,2560]{3,2,0,1:T(8,128)(2,1)S(1)}, u32[]{:S(2)}, u32[]{:S(2)}) %collective-permute-start.8) | collective-permute-done | bytes 1638432 | tf_op jit(solution)/shard_map/ppermute | solution.py:71
  360.8 24.1 %convolution_convert_fusion = bf16[1280,5120]{1,0:T(8,128)(2,1)S(1)} fusion(bf16[1536,1280]{1,0:T(8,128)(2,1)S(1)} %copy-done.8, bf16[1536,5120]{1,0:T(8,128)(2,1)} %get-tuple-element.368), kind=kOutput, calls=%fused_computation.18 | convolution fusion | flops 20139212800 | bytes 32768000 | tf_op jit(solution)/shard_map/dot_general | solution.py:42
  410.9 12.9 collective-permute-done.23
  436.8 26.9 %collective-permute-done.21 = bf16[4,2,160,640]{3,2,0,1:T(8,128)(2,1)S(1)} collective-permute-done((bf16[4,2,160,640]{3,2,0,1:T(8,128)(2,1)}, bf16[4,2,160,640]{3,2,0,1:T(8,128)(2,1)S(1)}, u32[]{:S(2)}, u32[]{:S(2)}) %collective-permute-start.21) | collective-permute-done | bytes 1638432 | tf_op jit(solution)/shard_map/ppermute | solution.py:71
  467.2 28.8 %collective-permute-done.22 = bf16[4,2,160,640]{3,2,0,1:T(8,128)(2,1)S(1)} collective-permute-done((bf16[4,2,160,640]{3,2,0,1:T(8,128)(2,1)}, bf16[4,2,160,640]{3,2,0,1:T(8,128)(2,1)S(1)}, u32[]{:S(2)}, u32[]{:S(2)}) %collective-permute-start.22) | collective-permute-done | bytes 1638432 | tf_op jit(solution)/shard_map/ppermute | solution.py:71
  508.2 10.8 collective-permute-done.15
  519.0 15.6 %collective-permute-done.16 = bf16[4,2,40,1280]{3,2,0,1:T(8,128)(2,1)S(1)} collective-permute-done((bf16[4,2,40,1280]{3,2,0,1:T(8,128)(2,1)S(1)}, bf16[4,2,40,1280]{3,2,0,1:T(8,128)(2,1)S(1)}, u32[]{:S(2)}, u32[]{:S(2)}) %collective-permute-start.16) | collective-permute-done | bytes 819232 | tf_op jit(solution)/shard_map/ppermute | solution.py:71
  545.1 16.8 %collective-permute-done.28 = bf16[4,2,40,1280]{3,2,0,1:T(8,128)(2,1)S(1)} collective-permute-done((bf16[4,2,40,1280]{3,2,0,1:T(8,128)(2,1)S(1)}, bf16[4,2,40,1280]{3,2,0,1:T(8,128)(2,1)S(1)}, u32[]{:S(2)}, u32[]{:S(2)}) %collective-permute-start.28) | collective-permute-done | bytes 819232 | tf_op jit(solution)/shard_map/ppermute | solution.py:71
  562.5 17.9 %collective-permute-done.27 = bf16[4,2,40,1280]{3,2,0,1:T(8,128)(2,1)S(1)} collective-permute-done((bf16[4,2,40,1280]{3,2,0,1:T(8,128)(2,1)S(1)}, bf16[4,2,40,1280]{3,2,0,1:T(8,128)(2,1)S(1)}, u32[]{:S(2)}, u32[]{:S(2)}) %collective-permute-start.27) | collective-permute-done | bytes 819232 | tf_op jit(solution)/shard_map/ppermute | solution.py:71
  586.2 19.1 %collective-permute-done.30 = bf16[4,2,40,1280]{3,2,0,1:T(8,128)(2,1)S(1)} collective-permute-done((bf16[4,2,40,1280]{3,2,0,1:T(8,128)(2,1)S(1)}, bf16[4,2,40,1280]{3,2,0,1:T(8,128)(2,1)S(1)}, u32[]{:S(2)}, u32[]{:S(2)}) %collective-permute-start.30) | collective-permute-done | bytes 819232 | tf_op jit(solution)/shard_map/ppermute | solution.py:71
  605.5 19.8 %collective-permute-done.31 = bf16[4,2,40,1280]{3,2,0,1:T(8,128)(2,1)S(1)} collective-permute-done((bf16[4,2,40,1280]{3,2,0,1:T(8,128)(2,1)S(1)}, bf16[4,2,40,1280]{3,2,0,1:T(8,128)(2,1)S(1)}, u32[]{:S(2)}, u32[]{:S(2)}) %collective-permute-start.31) | collective-permute-done | bytes 819232 | tf_op jit(solution)/shard_map/ppermute | solution.py:71
  632.6 12.5 collective-permute-done.25
  654.9 38.1 %collective-permute-done.58 = f32[160,1280]{1,0:T(8,128)S(1)} collective-permute-done((f32[160,1280]{1,0:T(8,128)S(1)}, f32[160,1280]{1,0:T(8,128)S(1)}, u32[]{:S(2)}, u32[]{:S(2)}) %collective-permute-start.58) | collective-permute-done | bytes 819232 | tf_op jit(solution)/shard_map/ppermute | solution.py:71
  693.1 18.1 %collective-permute-start.51 = (f32[40,2560]{1,0:T(8,128)S(1)}, f32[40,2560]{1,0:T(8,128)S(1)}, u32[]{:S(2)}, u32[]{:S(2)}) collective-permute-start(f32[40,2560]{1,0:T(8,128)S(1)} %copy-done.83), channel_id=1, source_target_pairs={{0,8},{1,9},{2,10},{3,11},{4,12},{5,13},{6,14},{7,15},{8,0},{9,1},... | collective-permute-start | bytes 1228808 | tf_op jit(solution)/shard_map/ppermute | solution.py:71
  721.9 24.4 %collective-permute-start.48 = (f32[160,640]{1,0:T(8,128)S(1)}, f32[160,640]{1,0:T(8,128)S(1)}, u32[]{:S(2)}, u32[]{:S(2)}) collective-permute-start(f32[160,640]{1,0:T(8,128)S(1)} %get-tuple-element.693), channel_id=1, source_target_pairs={{0,8},{1,9},{2,10},{3,11},{4,12},{5,13},{6,14},{7,15},{8,0},{9,1},... | collective-permute-start | bytes 1228808 | tf_op jit(solution)/shard_map/ppermute | solution.py:71
  758.6 22.8 %collective-permute-start.45 = (f32[160,640]{1,0:T(8,128)S(1)}, f32[160,640]{1,0:T(8,128)S(1)}, u32[]{:S(2)}, u32[]{:S(2)}) collective-permute-start(f32[160,640]{1,0:T(8,128)S(1)} %get-tuple-element.696), channel_id=1, source_target_pairs={{0,8},{1,9},{2,10},{3,11},{4,12},{5,13},{6,14},{7,15},{8,0},{9,1},... | collective-permute-start | bytes 1228808 | tf_op jit(solution)/shard_map/ppermute | solution.py:71
  792.2 15.6 %collective-permute-start.41 = (f32[40,1280]{1,0:T(8,128)S(1)}, f32[40,1280]{1,0:T(8,128)S(1)}, u32[]{:S(2)}, u32[]{:S(2)}) collective-permute-start(f32[40,1280]{1,0:T(8,128)S(1)} %get-tuple-element.715), channel_id=1, source_target_pairs={{0,8},{1,9},{2,10},{3,11},{4,12},{5,13},{6,14},{7,15},{8,0},{9,1},... | collective-permute-start | bytes 614408 | tf_op jit(solution)/shard_map/ppermute | solution.py:71
  819.4 15.9 %collective-permute-done.44 = f32[4,40,1280]{2,1,0:T(8,128)S(1)} collective-permute-done((f32[4,40,1280]{2,1,0:T(8,128)S(1)}, f32[4,40,1280]{2,1,0:T(8,128)S(1)}, u32[]{:S(2)}, u32[]{:S(2)}) %collective-permute-start.44) | collective-permute-done | bytes 819232 | tf_op jit(solution)/shard_map/ppermute | solution.py:71
  853.1 13.8 %collective-permute-done.38 = f32[40,1280]{1,0:T(8,128)S(1)} collective-permute-done((f32[40,1280]{1,0:T(8,128)S(1)}, f32[40,1280]{1,0:T(8,128)S(1)}, u32[]{:S(2)}, u32[]{:S(2)}) %collective-permute-start.38) | collective-permute-done | bytes 204832 | tf_op jit(solution)/shard_map/ppermute | solution.py:71
  878.5 10.9 collective-permute-done.65
  934.7 9.3 collective-permute-start.74
  963.0 14.4 %collective-permute-done.81 = bf16[4,40,2560]{2,1,0:T(8,128)(2,1)S(1)} collective-permute-done((bf16[4,40,2560]{2,1,0:T(8,128)(2,1)S(1)}, bf16[4,40,2560]{2,1,0:T(8,128)(2,1)S(1)}, u32[]{:S(2)}, u32[]{:S(2)}) %collective-permute-start.81) | collective-permute-done | bytes 819232 | tf_op jit(solution)/shard_map/ppermute | solution.py:71
  992.6 12.7 collective-permute-done.88
  1023.1 11.0 collective-permute-done.101
  1075.1 8.8 shard_map.183.refs_0_
  1084.0 8.8 shard_map.184
  1092.8 9.8 collective-permute-done.103.far
  1105.3 34.2 %fusion.7 = bf16[1536,5120]{1,0:T(8,128)(2,1)} fusion(bf16[1536,1280]{1,0:T(8,128)(2,1)} %bitcast.562, bf16[1280,5120]{1,0:T(8,128)(2,1)} %bitcast.462), kind=kOutput, calls=%fused_computation.9 | convolution fusion | flops 20203438080 | bytes 32768000 | tf_op jit(solution)/shard_map/dot_general | solution.py:42
  1151.7 8.4 collective-permute-done.109
  1174.5 8.8 shard_map.185.refs_0_
  1183.3 8.8 shard_map.186
  1192.1 28.2 %fusion.17 = bf16[1536,1280]{1,0:T(8,128)(2,1)} fusion(bf16[1536,5120]{1,0:T(8,128)(2,1)} %fusion.7, bf16[5120,1280]{1,0:T(8,128)(2,1)} %bitcast.463, bf16[1536,1280]{1,0:T(8,128)(2,1)} %bitcast.563), kind=kOutput, calls=%fused_computation.28 | convolution fusion | flops 20138557440 | bytes 36700160 | tf_op jit(solution)/shard_map/dot_general | solution.py:42
  1227.8 18.3 %collective-permute-done.122 = bf16[4,160,640]{2,1,0:T(8,128)(2,1)S(1)} collective-permute-done((bf16[4,160,640]{2,1,0:T(8,128)(2,1)S(1)}, bf16[4,160,640]{2,1,0:T(8,128)(2,1)S(1)}, u32[]{:S(2)}, u32[]{:S(2)}) %collective-permute-start.122) | collective-permute-done | bytes 819232 | tf_op jit(solution)/shard_map/ppermute | solution.py:71
  1251.0 8.8 shard_map.187.refs_0_
  1259.8 8.7 shard_map.188
  1268.5 34.4 %fusion.15 = bf16[1536,5120]{1,0:T(8,128)(2,1)} fusion(bf16[1536,1280]{1,0:T(8,128)(2,1)} %fusion.17, bf16[1280,5120]{1,0:T(8,128)(2,1)} %bitcast.464), kind=kOutput, calls=%fused_computation.17 | convolution fusion | flops 20203438080 | bytes 32768000 | tf_op jit(solution)/shard_map/dot_general | solution.py:42
  1309.1 8.8 shard_map.189.refs_0_
  1318.0 8.8 shard_map.190
  1326.8 28.1 %fusion.19 = bf16[1,1536,1280]{2,1,0:T(8,128)(2,1)} fusion(bf16[1536,5120]{1,0:T(8,128)(2,1)} %fusion.15, bf16[5120,1280]{1,0:T(8,128)(2,1)} %bitcast.461, bf16[1536,1280]{1,0:T(8,128)(2,1)} %fusion.17), kind=kOutput, calls=%fused_computation.30 | convolution fusion | flops 20138557440 | bytes 36700160 | tf_op jit(solution)/shard_map/dot_general | solution.py:42
  (606 shorter events, 432.6 us)
Async XLA Ops:
  49.5 165.7 %collective-permute-start = (bf16[2,2,160,1280]{3,2,0,1:T(8,128)(2,1)}, bf16[2,2,160,1280]{3,2,0,1:T(8,128)(2,1)}, u32[]{:S(2)}, u32[]{:S(2)}) collective-permute-start(bf16[2,2,160,1280]{3,2,0,1:T(8,128)(2,1)} %bitcast.447), channel_id=1, source_target_pairs={{0,1},{1,0},{2,3},{3,2},{4,5},{5,4},{6,7},{7,6},{8,9},{9,8},{10,11... | collective-permute-start | bytes 4915208 | tf_op jit(solution)/shard_map/ppermute | solution.py:71
  51.2 164.7 %collective-permute-start.1 = (bf16[2,2,160,1280]{3,2,0,1:T(8,128)(2,1)}, bf16[2,2,160,1280]{3,2,0,1:T(8,128)(2,1)}, u32[]{:S(2)}, u32[]{:S(2)}) collective-permute-start(bf16[2,2,160,1280]{3,2,0,1:T(8,128)(2,1)} %bitcast.446), channel_id=1, source_target_pairs={{0,2},{1,3},{2,0},{3,1},{4,6},{5,7},{6,4},{7,5},{8,10},{9,11},{10,... | collective-permute-start | bytes 4915208 | tf_op jit(solution)/shard_map/ppermute | solution.py:71
  55.0 162.7 %collective-permute-start.2 = (bf16[2,2,160,1280]{3,2,0,1:T(8,128)(2,1)}, bf16[2,2,160,1280]{3,2,0,1:T(8,128)(2,1)}, u32[]{:S(2)}, u32[]{:S(2)}) collective-permute-start(bf16[2,2,160,1280]{3,2,0,1:T(8,128)(2,1)} %bitcast.445), channel_id=1, source_target_pairs={{0,3},{1,2},{2,1},{3,0},{4,7},{5,6},{6,5},{7,4},{8,11},{9,10},{10,... | collective-permute-start | bytes 4915208 | tf_op jit(solution)/shard_map/ppermute | solution.py:71
  104.9 170.7 %collective-permute-start.9 = (bf16[2,2,160,1280]{3,2,0,1:T(8,128)(2,1)}, bf16[2,2,160,1280]{3,2,0,1:T(8,128)(2,1)}, u32[]{:S(2)}, u32[]{:S(2)}) collective-permute-start(bf16[2,2,160,1280]{3,2,0,1:T(8,128)(2,1)} %bitcast.444), channel_id=1, source_target_pairs={{0,1},{1,0},{2,3},{3,2},{4,5},{5,4},{6,7},{7,6},{8,9},{9,8},{10,11... | collective-permute-start | bytes 4915208 | tf_op jit(solution)/shard_map/ppermute | solution.py:71
  106.3 169.8 %collective-permute-start.10 = (bf16[2,2,160,1280]{3,2,0,1:T(8,128)(2,1)}, bf16[2,2,160,1280]{3,2,0,1:T(8,128)(2,1)}, u32[]{:S(2)}, u32[]{:S(2)}) collective-permute-start(bf16[2,2,160,1280]{3,2,0,1:T(8,128)(2,1)} %bitcast.443), channel_id=1, source_target_pairs={{0,4},{1,5},{2,6},{3,7},{4,0},{5,1},{6,2},{7,3},{8,12},{9,13},{10,... | collective-permute-start | bytes 4915208 | tf_op jit(solution)/shard_map/ppermute | solution.py:71
  215.9 60.4 %collective-permute-start.11 = (bf16[2,2,160,1280]{3,2,0,1:T(8,128)(2,1)S(1)}, bf16[2,2,160,1280]{3,2,0,1:T(8,128)(2,1)S(1)}, u32[]{:S(2)}, u32[]{:S(2)}) collective-permute-start(bf16[2,2,160,1280]{3,2,0,1:T(8,128)(2,1)S(1)} %bitcast.517), channel_id=1, source_target_pairs={{0,5},{1,4},{2,7},{3,6},{4,1},{5,0},{6,3},{7,2},{8,13},{9,12},{10,... | collective-permute-start | bytes 4915208 | tf_op jit(solution)/shard_map/ppermute | solution.py:71
  215.9 141.0 %collective-permute-start.5 = (bf16[4,2,40,2560]{3,2,0,1:T(8,128)(2,1)}, bf16[4,2,40,2560]{3,2,0,1:T(8,128)(2,1)}, u32[]{:S(2)}, u32[]{:S(2)}) collective-permute-start(bf16[4,2,40,2560]{3,2,0,1:T(8,128)(2,1)} %get-tuple-element.677), channel_id=1, source_target_pairs={{0,5},{1,4},{2,7},{3,6},{4,1},{5,0},{6,3},{7,2},{8,13},{9,12},{10,... | collective-permute-start | bytes 4915208 | tf_op jit(solution)/shard_map/ppermute | solution.py:71
  217.6 63.4 %collective-permute-start.6 = (bf16[4,2,40,2560]{3,2,0,1:T(8,128)(2,1)}, bf16[4,2,40,2560]{3,2,0,1:T(8,128)(2,1)S(1)}, u32[]{:S(2)}, u32[]{:S(2)}) collective-permute-start(bf16[4,2,40,2560]{3,2,0,1:T(8,128)(2,1)} %bitcast.441), channel_id=1, source_target_pairs={{0,1},{1,0},{2,3},{3,2},{4,5},{5,4},{6,7},{7,6},{8,9},{9,8},{10,11... | collective-permute-start | bytes 4915208 | tf_op jit(solution)/shard_map/ppermute | solution.py:71
  275.6 81.2 %collective-permute-start.4 = (bf16[4,2,40,2560]{3,2,0,1:T(8,128)(2,1)}, bf16[4,2,40,2560]{3,2,0,1:T(8,128)(2,1)S(1)}, u32[]{:S(2)}, u32[]{:S(2)}) collective-permute-start(bf16[4,2,40,2560]{3,2,0,1:T(8,128)(2,1)} %get-tuple-element.678), channel_id=1, source_target_pairs={{0,4},{1,5},{2,6},{3,7},{4,0},{5,1},{6,2},{7,3},{8,12},{9,13},{10,... | collective-permute-start | bytes 4915208 | tf_op jit(solution)/shard_map/ppermute | solution.py:71
  276.2 80.7 %collective-permute-start.3 = (bf16[4,2,40,2560]{3,2,0,1:T(8,128)(2,1)}, bf16[4,2,40,2560]{3,2,0,1:T(8,128)(2,1)S(1)}, u32[]{:S(2)}, u32[]{:S(2)}) collective-permute-start(bf16[4,2,40,2560]{3,2,0,1:T(8,128)(2,1)} %get-tuple-element.679), channel_id=1, source_target_pairs={{0,1},{1,0},{2,3},{3,2},{4,5},{5,4},{6,7},{7,6},{8,9},{9,8},{10,11... | collective-permute-start | bytes 4915208 | tf_op jit(solution)/shard_map/ppermute | solution.py:71
  281.0 68.1 %collective-permute-start.8 = (bf16[4,2,40,2560]{3,2,0,1:T(8,128)(2,1)S(1)}, bf16[4,2,40,2560]{3,2,0,1:T(8,128)(2,1)S(1)}, u32[]{:S(2)}, u32[]{:S(2)}) collective-permute-start(bf16[4,2,40,2560]{3,2,0,1:T(8,128)(2,1)S(1)} %bitcast.516), channel_id=1, source_target_pairs={{0,3},{1,2},{2,1},{3,0},{4,7},{5,6},{6,5},{7,4},{8,11},{9,10},{10,... | collective-permute-start | bytes 4915208 | tf_op jit(solution)/shard_map/ppermute | solution.py:71
  315.2 89.8 %collective-permute-start.12 = (f32[2,160,1280]{2,1,0:T(8,128)}, f32[2,160,1280]{2,1,0:T(8,128)}, u32[]{:S(2)}, u32[]{:S(2)}) collective-permute-start(f32[2,160,1280]{2,1,0:T(8,128)} %add_bitcast_fusion.5), channel_id=1, source_target_pairs={{0,4},{1,5},{2,6},{3,7},{4,0},{5,1},{6,2},{7,3},{8,12},{9,13},{10,... | collective-permute-start | bytes 4915208 | tf_op jit(solution)/shard_map/ppermute | solution.py:71
  349.1 56.4 %collective-permute-start.13 = (f32[2,160,1280]{2,1,0:T(8,128)}, f32[2,160,1280]{2,1,0:T(8,128)}, u32[]{:S(2)}, u32[]{:S(2)}) collective-permute-start(f32[2,160,1280]{2,1,0:T(8,128)} %add_bitcast_fusion.4), channel_id=1, source_target_pairs={{0,2},{1,3},{2,0},{3,1},{4,6},{5,7},{6,4},{7,5},{8,10},{9,11},{10,... | collective-permute-start | bytes 4915208 | tf_op jit(solution)/shard_map/ppermute | solution.py:71
  405.0 92.6 %collective-permute-start.19 = (bf16[4,2,160,640]{3,2,0,1:T(8,128)(2,1)}, bf16[4,2,160,640]{3,2,0,1:T(8,128)(2,1)S(1)}, u32[]{:S(2)}, u32[]{:S(2)}) collective-permute-start(bf16[4,2,160,640]{3,2,0,1:T(8,128)(2,1)} %get-tuple-element.671), channel_id=1, source_target_pairs={{0,5},{1,4},{2,7},{3,6},{4,1},{5,0},{6,3},{7,2},{8,13},{9,12},{10,... | collective-permute-start | bytes 4915208 | tf_op jit(solution)/shard_map/ppermute | solution.py:71
  405.5 92.9 %collective-permute-start.18 = (bf16[4,2,160,640]{3,2,0,1:T(8,128)(2,1)}, bf16[4,2,160,640]{3,2,0,1:T(8,128)(2,1)S(1)}, u32[]{:S(2)}, u32[]{:S(2)}) collective-permute-start(bf16[4,2,160,640]{3,2,0,1:T(8,128)(2,1)} %get-tuple-element.672), channel_id=1, source_target_pairs={{0,4},{1,5},{2,6},{3,7},{4,0},{5,1},{6,2},{7,3},{8,12},{9,13},{10,... | collective-permute-start | bytes 4915208 | tf_op jit(solution)/shard_map/ppermute | solution.py:71
  423.8 75.2 %collective-permute-start.17 = (bf16[4,2,160,640]{3,2,0,1:T(8,128)(2,1)}, bf16[4,2,160,640]{3,2,0,1:T(8,128)(2,1)S(1)}, u32[]{:S(2)}, u32[]{:S(2)}) collective-permute-start(bf16[4,2,160,640]{3,2,0,1:T(8,128)(2,1)} %get-tuple-element.673), channel_id=1, source_target_pairs={{0,1},{1,0},{2,3},{3,2},{4,5},{5,4},{6,7},{7,6},{8,9},{9,8},{10,11... | collective-permute-start | bytes 4915208 | tf_op jit(solution)/shard_map/ppermute | solution.py:71
  426.2 69.8 %collective-permute-start.22 = (bf16[4,2,160,640]{3,2,0,1:T(8,128)(2,1)}, bf16[4,2,160,640]{3,2,0,1:T(8,128)(2,1)S(1)}, u32[]{:S(2)}, u32[]{:S(2)}) collective-permute-start(bf16[4,2,160,640]{3,2,0,1:T(8,128)(2,1)} %bitcast.436), channel_id=1, source_target_pairs={{0,3},{1,2},{2,1},{3,0},{4,7},{5,6},{6,5},{7,4},{8,11},{9,10},{10,... | collective-permute-start | bytes 4915208 | tf_op jit(solution)/shard_map/ppermute | solution.py:71
  463.6 187.1 %collective-permute-start.59 = (f32[160,1280]{1,0:T(8,128)}, f32[160,1280]{1,0:T(8,128)}, u32[]{:S(2)}, u32[]{:S(2)}) collective-permute-start(f32[160,1280]{1,0:T(8,128)} %get-tuple-element.703), channel_id=1, source_target_pairs={{0,24},{1,25},{2,26},{3,27},{4,28},{5,29},{6,30},{7,31},{8,16},{9,... | collective-permute-start | bytes 2457608 | tf_op jit(solution)/shard_map/ppermute | solution.py:71
  537.5 115.0 %collective-permute-start.57 = (f32[160,1280]{1,0:T(8,128)S(1)}, f32[160,1280]{1,0:T(8,128)S(1)}, u32[]{:S(2)}, u32[]{:S(2)}) collective-permute-start(f32[160,1280]{1,0:T(8,128)S(1)} %copy-done.68), channel_id=1, source_target_pairs={{0,8},{1,9},{2,10},{3,11},{4,12},{5,13},{6,14},{7,15},{8,0},{9,1},... | collective-permute-start | bytes 2457608 | tf_op jit(solution)/shard_map/ppermute | solution.py:71
  544.3 86.3 %collective-permute-start.32 = (f32[4,160,640]{2,1,0:T(8,128)S(1)}, f32[4,160,640]{2,1,0:T(8,128)S(1)}, u32[]{:S(2)}, u32[]{:S(2)}) collective-permute-start(f32[4,160,640]{2,1,0:T(8,128)S(1)} %add_bitcast_fusion), channel_id=1, source_target_pairs={{0,2},{1,3},{2,0},{3,1},{4,6},{5,7},{6,4},{7,5},{8,10},{9,11},{10,... | collective-permute-start | bytes 4915208 | tf_op jit(solution)/shard_map/ppermute | solution.py:71
  561.9 65.3 %collective-permute-start.33 = (f32[4,160,640]{2,1,0:T(8,128)S(1)}, f32[4,160,640]{2,1,0:T(8,128)S(1)}, u32[]{:S(2)}, u32[]{:S(2)}) collective-permute-start(f32[4,160,640]{2,1,0:T(8,128)S(1)} %add_bitcast_fusion.1), channel_id=1, source_target_pairs={{0,4},{1,5},{2,6},{3,7},{4,0},{5,1},{6,2},{7,3},{8,12},{9,13},{10,... | collective-permute-start | bytes 4915208 | tf_op jit(solution)/shard_map/ppermute | solution.py:71
  627.2 65.8 %collective-permute-start.58 = (f32[160,1280]{1,0:T(8,128)S(1)}, f32[160,1280]{1,0:T(8,128)S(1)}, u32[]{:S(2)}, u32[]{:S(2)}) collective-permute-start(f32[160,1280]{1,0:T(8,128)S(1)} %copy-done.67), channel_id=1, source_target_pairs={{0,16},{1,17},{2,18},{3,19},{4,20},{5,21},{6,22},{7,23},{8,24},{9,... | collective-permute-start | bytes 2457608 | tf_op jit(solution)/shard_map/ppermute | solution.py:71
  649.8 69.6 %collective-permute-start.55 = (f32[40,2560]{1,0:T(8,128)S(1)}, f32[40,2560]{1,0:T(8,128)S(1)}, u32[]{:S(2)}, u32[]{:S(2)}) collective-permute-start(f32[40,2560]{1,0:T(8,128)S(1)} %copy-done.87), channel_id=1, source_target_pairs={{0,16},{1,17},{2,18},{3,19},{4,20},{5,21},{6,22},{7,23},{8,24},{9,... | collective-permute-start | bytes 1228808 | tf_op jit(solution)/shard_map/ppermute | solution.py:71
  650.8 71.1 %collective-permute-start.54 = (f32[40,2560]{1,0:T(8,128)S(1)}, f32[40,2560]{1,0:T(8,128)S(1)}, u32[]{:S(2)}, u32[]{:S(2)}) collective-permute-start(f32[40,2560]{1,0:T(8,128)S(1)} %copy-done.86), channel_id=1, source_target_pairs={{0,8},{1,9},{2,10},{3,11},{4,12},{5,13},{6,14},{7,15},{8,0},{9,1},... | collective-permute-start | bytes 1228808 | tf_op jit(solution)/shard_map/ppermute | solution.py:71
  652.4 69.5 %collective-permute-start.53 = (f32[40,2560]{1,0:T(8,128)S(1)}, f32[40,2560]{1,0:T(8,128)S(1)}, u32[]{:S(2)}, u32[]{:S(2)}) collective-permute-start(f32[40,2560]{1,0:T(8,128)S(1)} %copy-done.85), channel_id=1, source_target_pairs={{0,24},{1,25},{2,26},{3,27},{4,28},{5,29},{6,30},{7,31},{8,16},{9,... | collective-permute-start | bytes 1228808 | tf_op jit(solution)/shard_map/ppermute | solution.py:71
  693.0 61.5 %collective-permute-start.52 = (f32[40,2560]{1,0:T(8,128)S(1)}, f32[40,2560]{1,0:T(8,128)S(1)}, u32[]{:S(2)}, u32[]{:S(2)}) collective-permute-start(f32[40,2560]{1,0:T(8,128)S(1)} %copy-done.84), channel_id=1, source_target_pairs={{0,16},{1,17},{2,18},{3,19},{4,20},{5,21},{6,22},{7,23},{8,24},{9,... | collective-permute-start | bytes 1228808 | tf_op jit(solution)/shard_map/ppermute | solution.py:71
  693.1 63.9 %collective-permute-start.51 = (f32[40,2560]{1,0:T(8,128)S(1)}, f32[40,2560]{1,0:T(8,128)S(1)}, u32[]{:S(2)}, u32[]{:S(2)}) collective-permute-start(f32[40,2560]{1,0:T(8,128)S(1)} %copy-done.83), channel_id=1, source_target_pairs={{0,8},{1,9},{2,10},{3,11},{4,12},{5,13},{6,14},{7,15},{8,0},{9,1},... | collective-permute-start | bytes 1228808 | tf_op jit(solution)/shard_map/ppermute | solution.py:71
  721.9 67.8 %collective-permute-start.49 = (f32[160,640]{1,0:T(8,128)S(1)}, f32[160,640]{1,0:T(8,128)S(1)}, u32[]{:S(2)}, u32[]{:S(2)}) collective-permute-start(f32[160,640]{1,0:T(8,128)S(1)} %get-tuple-element.692), channel_id=1, source_target_pairs={{0,16},{1,17},{2,18},{3,19},{4,20},{5,21},{6,22},{7,23},{8,24},{9,... | collective-permute-start | bytes 1228808 | tf_op jit(solution)/shard_map/ppermute | solution.py:71
  721.9 70.3 %collective-permute-start.48 = (f32[160,640]{1,0:T(8,128)S(1)}, f32[160,640]{1,0:T(8,128)S(1)}, u32[]{:S(2)}, u32[]{:S(2)}) collective-permute-start(f32[160,640]{1,0:T(8,128)S(1)} %get-tuple-element.693), channel_id=1, source_target_pairs={{0,8},{1,9},{2,10},{3,11},{4,12},{5,13},{6,14},{7,15},{8,0},{9,1},... | collective-permute-start | bytes 1228808 | tf_op jit(solution)/shard_map/ppermute | solution.py:71
  757.0 59.1 %collective-permute-start.46 = (f32[160,640]{1,0:T(8,128)S(1)}, f32[160,640]{1,0:T(8,128)S(1)}, u32[]{:S(2)}, u32[]{:S(2)}) collective-permute-start(f32[160,640]{1,0:T(8,128)S(1)} %get-tuple-element.695), channel_id=1, source_target_pairs={{0,16},{1,17},{2,18},{3,19},{4,20},{5,21},{6,22},{7,23},{8,24},{9,... | collective-permute-start | bytes 1228808 | tf_op jit(solution)/shard_map/ppermute | solution.py:71
  758.6 58.8 %collective-permute-start.45 = (f32[160,640]{1,0:T(8,128)S(1)}, f32[160,640]{1,0:T(8,128)S(1)}, u32[]{:S(2)}, u32[]{:S(2)}) collective-permute-start(f32[160,640]{1,0:T(8,128)S(1)} %get-tuple-element.696), channel_id=1, source_target_pairs={{0,8},{1,9},{2,10},{3,11},{4,12},{5,13},{6,14},{7,15},{8,0},{9,1},... | collective-permute-start | bytes 1228808 | tf_op jit(solution)/shard_map/ppermute | solution.py:71
  789.7 50.0 %collective-permute-start.43 = (f32[40,1280]{1,0:T(8,128)S(1)}, f32[40,1280]{1,0:T(8,128)S(1)}, u32[]{:S(2)}, u32[]{:S(2)}) collective-permute-start(f32[40,1280]{1,0:T(8,128)S(1)} %get-tuple-element.713), channel_id=1, source_target_pairs={{0,24},{1,25},{2,26},{3,27},{4,28},{5,29},{6,30},{7,31},{8,16},{9,... | collective-permute-start | bytes 614408 | tf_op jit(solution)/shard_map/ppermute | solution.py:71
  792.2 52.0 %collective-permute-start.41 = (f32[40,1280]{1,0:T(8,128)S(1)}, f32[40,1280]{1,0:T(8,128)S(1)}, u32[]{:S(2)}, u32[]{:S(2)}) collective-permute-start(f32[40,1280]{1,0:T(8,128)S(1)} %get-tuple-element.715), channel_id=1, source_target_pairs={{0,8},{1,9},{2,10},{3,11},{4,12},{5,13},{6,14},{7,15},{8,0},{9,1},... | collective-permute-start | bytes 614408 | tf_op jit(solution)/shard_map/ppermute | solution.py:71
  979.1 64.4 %collective-permute-start.83 = (bf16[2,4,40,2560]{3,2,1,0:T(8,128)(2,1)S(1)}, bf16[2,4,40,2560]{3,2,1,0:T(8,128)(2,1)S(1)}, u32[]{:S(2)}, u32[]{:S(2)}) collective-permute-start(bf16[2,4,40,2560]{3,2,1,0:T(8,128)(2,1)S(1)} %pad_maximum_fusion.1.own), channel_id=1, source_target_pairs={{0,4},{1,5},{2,6},{3,7},{4,0},{5,1},{6,2},{7,3},{8,12},{9,13},{10,... | collective-permute-start | bytes 4915208 | tf_op jit(solution)/shard_map/ppermute | solution.py:71
  980.8 65.7 %collective-permute-start.82 = (bf16[2,4,40,2560]{3,2,1,0:T(8,128)(2,1)S(1)}, bf16[2,4,40,2560]{3,2,1,0:T(8,128)(2,1)S(1)}, u32[]{:S(2)}, u32[]{:S(2)}) collective-permute-start(bf16[2,4,40,2560]{3,2,1,0:T(8,128)(2,1)S(1)} %pad_maximum_fusion.own), channel_id=1, source_target_pairs={{0,2},{1,3},{2,0},{3,1},{4,6},{5,7},{6,4},{7,5},{8,10},{9,11},{10,... | collective-permute-start | bytes 4915208 | tf_op jit(solution)/shard_map/ppermute | solution.py:71
  1008.4 56.9 %collective-permute-start.92 = (bf16[2,4,40,2560]{3,2,1,0:T(8,128)(2,1)S(1)}, bf16[2,4,40,2560]{3,2,1,0:T(8,128)(2,1)S(1)}, u32[]{:S(2)}, u32[]{:S(2)}) collective-permute-start(bf16[2,4,40,2560]{3,2,1,0:T(8,128)(2,1)S(1)} %pad_maximum_fusion.1.own), channel_id=1, source_target_pairs={{0,1},{1,0},{2,3},{3,2},{4,5},{5,4},{6,7},{7,6},{8,9},{9,8},{10,11... | collective-permute-start | bytes 4915208 | tf_op jit(solution)/shard_map/ppermute | solution.py:71
  1069.5 70.1 %collective-permute-start.113 = (bf16[160,640]{1,0:T(8,128)(2,1)S(1)}, bf16[160,640]{1,0:T(8,128)(2,1)}, u32[]{:S(2)}, u32[]{:S(2)}) collective-permute-start(bf16[160,640]{1,0:T(8,128)(2,1)S(1)} %get-tuple-element.587), channel_id=1, source_target_pairs={{0,24},{1,25},{2,26},{3,27},{4,28},{5,29},{6,30},{7,31},{8,16},{9,... | collective-permute-start | bytes 614408 | tf_op jit(solution)/shard_map/ppermute | solution.py:71
  1071.3 68.2 %collective-permute-start.112 = (bf16[160,640]{1,0:T(8,128)(2,1)S(1)}, bf16[160,640]{1,0:T(8,128)(2,1)}, u32[]{:S(2)}, u32[]{:S(2)}) collective-permute-start(bf16[160,640]{1,0:T(8,128)(2,1)S(1)} %get-tuple-element.587), channel_id=1, source_target_pairs={{0,16},{1,17},{2,18},{3,19},{4,20},{5,21},{6,22},{7,23},{8,24},{9,... | collective-permute-start | bytes 614408 | tf_op jit(solution)/shard_map/ppermute | solution.py:71
  1073.6 66.4 %collective-permute-start.111 = (bf16[160,640]{1,0:T(8,128)(2,1)S(1)}, bf16[160,640]{1,0:T(8,128)(2,1)}, u32[]{:S(2)}, u32[]{:S(2)}) collective-permute-start(bf16[160,640]{1,0:T(8,128)(2,1)S(1)} %get-tuple-element.587), channel_id=1, source_target_pairs={{0,8},{1,9},{2,10},{3,11},{4,12},{5,13},{6,14},{7,15},{8,0},{9,1},... | collective-permute-start | bytes 614408 | tf_op jit(solution)/shard_map/ppermute | solution.py:71
  1166.7 82.1 %collective-permute-start.120 = (bf16[2,4,40,2560]{3,2,1,0:T(8,128)(2,1)}, bf16[2,4,40,2560]{3,2,1,0:T(8,128)(2,1)}, u32[]{:S(2)}, u32[]{:S(2)}) collective-permute-start(bf16[2,4,40,2560]{3,2,1,0:T(8,128)(2,1)} %pad_maximum_fusion.5.own), channel_id=1, source_target_pairs={{0,1},{1,0},{2,3},{3,2},{4,5},{5,4},{6,7},{7,6},{8,9},{9,8},{10,11... | collective-permute-start | bytes 4915208 | tf_op jit(solution)/shard_map/ppermute | solution.py:71
  1169.9 50.4 %collective-permute-start.117 = (bf16[2,4,40,2560]{3,2,1,0:T(8,128)(2,1)}, bf16[2,4,40,2560]{3,2,1,0:T(8,128)(2,1)}, u32[]{:S(2)}, u32[]{:S(2)}) collective-permute-start(bf16[2,4,40,2560]{3,2,1,0:T(8,128)(2,1)} %pad_maximum_fusion.5.own), channel_id=1, source_target_pairs={{0,4},{1,5},{2,6},{3,7},{4,0},{5,1},{6,2},{7,3},{8,12},{9,13},{10,... | collective-permute-start | bytes 4915208 | tf_op jit(solution)/shard_map/ppermute | solution.py:71
  1170.7 79.4 %collective-permute-start.118 = (bf16[2,4,40,2560]{3,2,1,0:T(8,128)(2,1)S(1)}, bf16[2,4,40,2560]{3,2,1,0:T(8,128)(2,1)}, u32[]{:S(2)}, u32[]{:S(2)}) collective-permute-start(bf16[2,4,40,2560]{3,2,1,0:T(8,128)(2,1)S(1)} %pad_maximum_fusion.4.own), channel_id=1, source_target_pairs={{0,1},{1,0},{2,3},{3,2},{4,5},{5,4},{6,7},{7,6},{8,9},{9,8},{10,11... | collective-permute-start | bytes 4915208 | tf_op jit(solution)/shard_map/ppermute | solution.py:71
  1170.9 49.4 %collective-permute-start.116 = (bf16[2,4,40,2560]{3,2,1,0:T(8,128)(2,1)S(1)}, bf16[2,4,40,2560]{3,2,1,0:T(8,128)(2,1)}, u32[]{:S(2)}, u32[]{:S(2)}) collective-permute-start(bf16[2,4,40,2560]{3,2,1,0:T(8,128)(2,1)S(1)} %pad_maximum_fusion.4.own), channel_id=1, source_target_pairs={{0,2},{1,3},{2,0},{3,1},{4,6},{5,7},{6,4},{7,5},{8,10},{9,11},{10,... | collective-permute-start | bytes 4915208 | tf_op jit(solution)/shard_map/ppermute | solution.py:71
  1173.7 52.9 %collective-permute-start.123 = (bf16[4,160,640]{2,1,0:T(8,128)(2,1)}, bf16[4,160,640]{2,1,0:T(8,128)(2,1)S(1)}, u32[]{:S(2)}, u32[]{:S(2)}) collective-permute-start(bf16[4,160,640]{2,1,0:T(8,128)(2,1)} %pad_maximum_fusion.15), channel_id=1, source_target_pairs={{0,2},{1,3},{2,0},{3,1},{4,6},{5,7},{6,4},{7,5},{8,10},{9,11},{10,... | collective-permute-start | bytes 2457608 | tf_op jit(solution)/shard_map/ppermute | solution.py:71
  1248.6 54.9 %collective-permute-start.128 = (bf16[2,4,160,640]{3,2,1,0:T(8,128)(2,1)}, bf16[2,4,160,640]{3,2,1,0:T(8,128)(2,1)}, u32[]{:S(2)}, u32[]{:S(2)}) collective-permute-start(bf16[2,4,160,640]{3,2,1,0:T(8,128)(2,1)} %pad_maximum_fusion.7.own), channel_id=1, source_target_pairs={{0,1},{1,0},{2,3},{3,2},{4,5},{5,4},{6,7},{7,6},{8,9},{9,8},{10,11... | collective-permute-start | bytes 4915208 | tf_op jit(solution)/shard_map/ppermute | solution.py:71
  1248.8 54.1 %collective-permute-start.125 = (bf16[2,4,160,640]{3,2,1,0:T(8,128)(2,1)}, bf16[2,4,160,640]{3,2,1,0:T(8,128)(2,1)}, u32[]{:S(2)}, u32[]{:S(2)}) collective-permute-start(bf16[2,4,160,640]{3,2,1,0:T(8,128)(2,1)} %pad_maximum_fusion.7.own), channel_id=1, source_target_pairs={{0,4},{1,5},{2,6},{3,7},{4,0},{5,1},{6,2},{7,3},{8,12},{9,13},{10,... | collective-permute-start | bytes 4915208 | tf_op jit(solution)/shard_map/ppermute | solution.py:71
  1250.1 53.3 %collective-permute-start.126 = (bf16[2,4,160,640]{3,2,1,0:T(8,128)(2,1)S(1)}, bf16[2,4,160,640]{3,2,1,0:T(8,128)(2,1)S(1)}, u32[]{:S(2)}, u32[]{:S(2)}) collective-permute-start(bf16[2,4,160,640]{3,2,1,0:T(8,128)(2,1)S(1)} %pad_maximum_fusion.6.own), channel_id=1, source_target_pairs={{0,1},{1,0},{2,3},{3,2},{4,5},{5,4},{6,7},{7,6},{8,9},{9,8},{10,11... | collective-permute-start | bytes 4915208 | tf_op jit(solution)/shard_map/ppermute | solution.py:71
  1250.4 52.5 %collective-permute-start.124 = (bf16[2,4,160,640]{3,2,1,0:T(8,128)(2,1)S(1)}, bf16[2,4,160,640]{3,2,1,0:T(8,128)(2,1)}, u32[]{:S(2)}, u32[]{:S(2)}) collective-permute-start(bf16[2,4,160,640]{3,2,1,0:T(8,128)(2,1)S(1)} %pad_maximum_fusion.6.own), channel_id=1, source_target_pairs={{0,2},{1,3},{2,0},{3,1},{4,6},{5,7},{6,4},{7,5},{8,10},{9,11},{10,... | collective-permute-start | bytes 4915208 | tf_op jit(solution)/shard_map/ppermute | solution.py:71
  (179 other events, 3833.8 us)

commit v2 on v1

--- a/solution.py
+++ b/solution.py
@@ -25,10 +25,6 @@
 SIZES = {"z": 4, "y": 2, "x": 2, "c": 2}
 
 
-def gelu_fn(pre_act):
-    return jax.nn.gelu(pre_act, approximate=True)
-
-
 def adamw_update(master_old, mom_one, mom_two, grad_clip):
     mom_one_new = BETA_ONE * mom_one + (1.0 - BETA_ONE) * grad_clip
     mom_two_new = BETA_TWO * mom_two + (1.0 - BETA_TWO) * grad_clip * grad_clip
@@ -76,8 +72,8 @@
         self.place, self.order = place, order
         self.dims = ["z", "y", "x"]
         self.rows, self.depth = rows, depth
-        self.cols = cols or (0, part.shape[1])
-        self.part = part.reshape(depth, 2, 2, 2, rows, part.shape[1])
+        self.cols = (0, part.shape[1]) if cols is None else cols
+        self.part = None if part is None else part.reshape(depth, 2, 2, 2, rows, part.shape[1])
 
     def block(self, part, dim, flip, flip_core):
         sizes = [self.depth, 2, 2, 1, self.rows, self.cols[1] - self.cols[0]]
@@ -109,9 +105,8 @@
         axis = self.dims.index(dim)
         mine = self.place.at[dim]
         flips = range(1, SIZES[dim])
-        sends = self.place.chain.step(lambda terms: [self.total(terms, axis, mine ^ flip) for flip in flips], self.terms)
-        self.terms = [pick(term, axis, mine) for term in self.terms]
-        self.terms += [self.place.swap(send, flip * MASKS[dim]) for flip, send in zip(flips, sends)]
+        sends = self.place.chain.step(lambda terms: [self.total(terms, axis, mine ^ flip) for flip in range(SIZES[dim])], self.terms)
+        self.terms = [sends[0]] + [self.place.swap(sends[flip], flip * MASKS[dim]) for flip in flips]
         self.dims.remove(dim)
         self.stage += 1
 
@@ -119,20 +114,87 @@
         return self.total([term[None] for term in terms], 0, 0)
 
 
-class ReduceSplit:
-    def __init__(self, place, low, high):
-        self.place, self.low, self.high = place, low, high
-
-    def merge(self):
-        def both(terms):
-            whole = jnp.concatenate([self.low.sum(terms[0]), self.high.sum(terms[1])], axis=0)
-            return [pick(whole, 0, self.place.at["z"] ^ flip) for flip in range(4)]
-
-        sends = self.place.chain.step(both, (self.low.terms, self.high.terms))
-        self.terms = [sends[0]] + [self.place.swap(sends[flip], 8 * flip) for flip in (1, 2, 3)]
+class Merge:
+    def __init__(self, place, chunks, by_rows=False):
+        self.place = place
+        low = place.at["z"] & 1
+
+        def near(all_terms):
+            parts = [chunk.sum(terms) for chunk, terms in zip(chunks, all_terms)]
+            if by_rows:
+                whole = jnp.stack(parts)
+            else:
+                whole = jnp.concatenate(parts, axis=2)
+                whole = whole.reshape(2, 2, *whole.shape[1:])
+            return pick(whole, 1, low), pick(whole, 1, 1 - low)
+
+        own, send = place.chain.step(near, [chunk.terms for chunk in chunks])
+        self.terms = [own, place.swap(send, 8)]
+
+    def far(self):
+        high = self.place.at["z"] >> 1
+
+        def sends(terms):
+            total = terms[0] + terms[1]
+            return pick(total, 0, high), pick(total, 0, 1 - high)
+
+        own, send = self.place.chain.step(sends, self.terms)
+        self.terms = [own, self.place.swap(send, 16)]
 
     def sum(self, terms):
-        return sum(terms)
+        return terms[0] + terms[1]
+
+
+PACK_FLIPS = ((0, 0), (0, 1), (1, 0), (1, 1))
+
+
+def pack_kernel(orders, width, where, part, *outs):
+    core = where[3]
+    for i, order in enumerate(orders):
+        cols = pl.ds(i * width, width)
+        for j, (flip, flip_core) in enumerate(PACK_FLIPS):
+            out = outs[4 * i + j]
+            for k in (0, 1):
+                if order[0] == "x":
+                    out[k, 0] = part[0, k, where[2] ^ flip, core ^ flip_core, :, cols]
+                else:
+                    out[k, 0] = part[0, where[1] ^ flip, k, core ^ flip_core, :, cols]
+
+
+def pack(place, where, part, rows, orders):
+    total = part.shape[1]
+    width = total // len(orders)
+    part = part.reshape(4, 2, 2, 2, rows, total)
+    n_out = 4 * len(orders)
+    pieces = place.chain.step(lambda v: pl.pallas_call(
+        functools.partial(pack_kernel, orders, width),
+        grid_spec=pltpu.PrefetchScalarGridSpec(
+            num_scalar_prefetch=1,
+            grid=(4,),
+            in_specs=[pl.BlockSpec((1, 2, 2, 2, rows, total), lambda z, where: (z, 0, 0, 0, 0, 0))],
+            out_specs=[pl.BlockSpec((2, 1, rows, width), lambda z, where: (0, z, 0, 0))] * n_out,
+        ),
+        out_shape=[jax.ShapeDtypeStruct((2, 4, rows, width), BF16)] * n_out,
+        cost_estimate=pl.CostEstimate(flops=10 ** 9, bytes_accessed=4 * 32 * rows * total, transcendentals=0),
+        name="pack",
+    )(*v), (where, part))
+    chunks = []
+    for i, order in enumerate(orders):
+        chunk = Reduce(place, None, rows, order, (i * width, (i + 1) * width))
+        chunk.packed = pieces[4 * i:4 * i + 4]
+        chunks.append(chunk)
+    return chunks
+
+
+def send_first(chunks, hold=False):
+    packed = [chunk.packed for chunk in chunks]
+    if hold:
+        packed = chunks[0].place.chain.step(lambda v: v, packed)
+    for chunk, pieces in zip(chunks, packed):
+        dim = chunk.order[0]
+        chunk.terms = [pieces[0]] + [chunk.place.swap(piece, flip * MASKS[dim] + core) for (flip, core), piece in zip(PACK_FLIPS[1:], pieces[1:])]
+        chunk.dims = [chunk.order[1], "z"]
+        chunk.stage = 1
 
 
 def join_kernel(last, where, own, far, own_core, far_core, *refs):
@@ -140,10 +202,11 @@
     core = where[3]
     bit = where[{"y": 1, "x": 2}[last]]
     for ref, flip, flip_core in ((own, 0, 0), (far, 1, 0), (own_core, 0, 1), (far_core, 1, 1)):
-        if last == "x":
-            out[0, 0, bit ^ flip, core ^ flip_core] = ref[0, 0]
-        else:
-            out[0, bit ^ flip, 0, core ^ flip_core] = ref[0, 0]
+        for k in (0, 1):
+            if last == "x":
+                out[(where[0] & 1) ^ k, 0, bit ^ flip, core ^ flip_core] = ref[0, k]
+            else:
+                out[(where[0] & 1) ^ k, bit ^ flip, 0, core ^ flip_core] = ref[0, k]
 
 
 def join(last, where, pieces, whole, cols, half):
@@ -154,11 +217,11 @@
 
     def out_map(i, j, where):
         if last == "x":
-            return (where[0] ^ j, where[1] ^ i, 0, 0, 0, half)
-        return (where[0] ^ j, 0, where[2] ^ i, 0, 0, half)
-
-    block = (1, 1, 2, 2, rows, part) if last == "x" else (1, 2, 1, 2, rows, part)
-    in_specs = [pl.BlockSpec((1, 1, rows, part), in_map)] * 4
+            return ((where[0] >> 1) ^ j, where[1] ^ i, 0, 0, 0, half)
+        return ((where[0] >> 1) ^ j, 0, where[2] ^ i, 0, 0, half)
+
+    block = (2, 1, 2, 2, rows, part) if last == "x" else (2, 2, 1, 2, rows, part)
+    in_specs = [pl.BlockSpec((1, 2, rows, part), in_map)] * 4
     args = list(pieces)
     aliases = {}
     if whole is not None:
@@ -167,7 +230,7 @@
         aliases = {5: 0}
     return pl.pallas_call(
         functools.partial(join_kernel, last),
-        grid_spec=pltpu.PrefetchScalarGridSpec(num_scalar_prefetch=1, grid=(2, 4), in_specs=in_specs, out_specs=pl.BlockSpec(block, out_map)),
+        grid_spec=pltpu.PrefetchScalarGridSpec(num_scalar_prefetch=1, grid=(2, 2), in_specs=in_specs, out_specs=pl.BlockSpec(block, out_map)),
         out_shape=jax.ShapeDtypeStruct((4, 2, 2, 2, rows, cols), BF16),
         input_output_aliases=aliases,
         cost_estimate=pl.CostEstimate(flops=10 ** 9, bytes_accessed=8 * 8 * rows * part * 2, transcendentals=0),
@@ -182,12 +245,12 @@
         self.third = ["x", "y"]
 
     def send_z(self):
+        shard = self.place.chain.step(lambda shard: shard, self.shard)
+        self.shards = [shard] + [self.place.swap(shard, 8 * flip) for flip in (1, 2, 3)]
+
+    def send_second(self):
         half = self.cols // 2
-        pieces = self.place.chain.step(lambda shard: [shard[:, :half], shard[:, half:]], self.shard)
-        self.pieces = [[piece] + [self.place.swap(piece, 8 * flip) for flip in (1, 2, 3)] for piece in pieces]
-
-    def send_second(self):
-        stacks = self.place.chain.step(lambda pieces: [jnp.stack(piece) for piece in pieces], self.pieces)
+        stacks = self.place.chain.step(lambda shards: [jnp.stack([shard[:, i * half:(i + 1) * half] for shard in shards]) for i in (0, 1)], self.shards)
         self.pieces = [[stack, self.place.swap(stack, MASKS[dim])] for stack, dim in zip(stacks, self.second)]
 
     def send_third(self):
@@ -252,6 +315,40 @@
     )(*args)
 
 
+def act_kernel(n_split, x_ref, up_ref, *refs):
+    act_ref = refs[-1]
+    step = x_ref.shape[0] // n_split
+    for i in range(n_split):
+        rows = pl.ds(i * step, step)
+        h = dot(x_ref[rows, :], up_ref[...], 1, 0)
+        t = jnp.tanh(GELU_SCALE * h * (1.0 + GELU_CUBIC * (h * h)))
+        act_ref[rows, :] = (h * (0.5 * (1.0 + t))).astype(BF16)
+
+
+def hidden_act(x_in, w_up, part=0, n_parts=1, act=None):
+    tokens, width = x_in.shape
+    cols = w_up.shape[1]
+    tile = 512
+    steps = cols // tile
+    in_specs = [pl.BlockSpec((tokens, width), lambda j: (0, 0)), pl.BlockSpec((width, tile), lambda j: (0, j))]
+    args = [x_in, w_up]
+    aliases = {}
+    if act is not None:
+        in_specs.append(pl.BlockSpec(memory_space=pl.ANY))
+        args.append(act)
+        aliases = {2: 0}
+    return pl.pallas_call(
+        functools.partial(act_kernel, 6),
+        grid=(steps,),
+        in_specs=in_specs,
+        out_specs=pl.BlockSpec((tokens, tile), lambda j: (0, part * steps + j)),
+        out_shape=jax.ShapeDtypeStruct((tokens, cols * n_parts), BF16),
+        input_output_aliases=aliases,
+        compiler_params=pltpu.CompilerParams(vmem_limit_bytes=48 * 2 ** 20),
+        cost_estimate=pl.CostEstimate(flops=2 * tokens * width * cols, bytes_accessed=33 * 10 ** 6 // n_parts, transcendentals=tokens * cols),
+    )(*args)
+
+
 def total_square(value, place):
     value = value.reshape(1, 1)
     value = value + place.swap(value, 1) + place.swap(value, 2) + place.swap(value, 3)
@@ -275,101 +372,107 @@
         def weight_grad(pair):
             return dot(pair[0], pair[1], 0, 0).astype(BF16)
 
-        def split(part, rows, *orders):
-            cols = part.shape[1] // len(orders)
-            return [Reduce(place, part, rows, order, (i * cols, (i + 1) * cols)) for i, order in enumerate(orders)]
+        where = jnp.stack([place.at[d] for d in "zyxc"]).astype(jnp.int32)
+
+        def down_grad(act, grad):
+            return chain.step(lambda v: weight_grad((v, grad)), act)
+
+        def up_grad(layer, slopes):
+            return chain.step(lambda v: weight_grad((x_tokens[layer], v)), slopes)
 
         act_low, slopes = chain.step(lambda v: hidden_pair(1, *v, part=0, n_parts=2), (x_tokens, grad_two, w_up, w_down))
-        down_low = Reduce(place, chain.step(weight_grad, (act_low, grad_two)), rows_down, "xy", depth=2)
+        down_low = Reduce(place, down_grad(act_low, grad_two), rows_down, "xy", depth=2)
         down_low.first()
         act_high, pre_two = chain.step(lambda v: hidden_pair(1, *v[:4], part=1, n_parts=2, slopes=v[4]), (x_tokens, grad_two, w_up, w_down, slopes))
-        down_high = Reduce(place, chain.step(weight_grad, (act_high, grad_two)), rows_down, "yx", depth=2)
+        down_high = Reduce(place, down_grad(act_high, grad_two), rows_down, "yx", depth=2)
         down_high.first()
-        down_two = ReduceSplit(place, down_low, down_high)
-        up_two = split(chain.step(weight_grad, (x_tokens[1], pre_two)), rows_up, "xyz", "yxz")
-        for chunk in up_two:
-            chunk.first()
-        grad_one = chain.step(lambda v: (v[1].astype(F32) + dot(v[0], v[2], 1, 1)).astype(BF16), (pre_two, grad_two, w_up[1]))
+        up_two = pack(place, where, up_grad(1, pre_two), rows_up, ("xyz", "yxz"))
+        send_first(up_two)
         down_low.next()
+        grad_one = chain.step(lambda v: (grad_two.astype(F32) + dot(v, w_up[1], 1, 1)).astype(BF16), pre_two)
+        down_high.next()
         act_one, pre_one = chain.step(lambda v: hidden_pair(0, *v), (x_tokens, grad_one, w_up, w_down))
-        down_high.next()
-        down_one = split(chain.step(weight_grad, (act_one, grad_one)), rows_down, "xyz", "yxz")
-        for chunk in down_one:
-            chunk.first()
         for chunk in up_two:
             chunk.next()
-        up_one = split(chain.step(weight_grad, (x_tokens[0], pre_one)), rows_up, "xyz", "yxz", "xyz", "yxz")
-        down_two.merge()
-        up_one[0].first()
-        up_one[1].first()
-        for chunk in up_two:
-            chunk.next()
+        down_one = pack(place, where, down_grad(act_one, grad_one), rows_down, ("xyz", "yxz"))
+        send_first(down_one)
+        down_two = Merge(place, [down_low, down_high], True)
+        up_one = pack(place, where, up_grad(0, pre_one), rows_up, ("xyz", "yxz", "xyz", "yxz"))
+        send_first(up_one[:2])
+        down_two.far()
+        up_two = Merge(place, up_two)
         for chunk in down_one:
             chunk.next()
-        up_one[2].first()
-        up_one[3].first()
+        up_two.far()
         up_one[0].next()
         up_one[1].next()
-        for chunk in down_one:
-            chunk.next()
+        send_first(up_one[2:], hold=True)
+        down_one = Merge(place, down_one)
+        up_one_left = Merge(place, up_one[:2])
+        down_one.far()
+        up_one_left.far()
         up_one[2].next()
         up_one[3].next()
-
-        def grads_of(chunks):
-            def add(values):
-                terms, gacc = values
+        up_one_right = Merge(place, up_one[2:])
+
+        def grads_of(chunks, gacc):
+            def add(terms):
                 sums = [chunk.sum(term) for chunk, term in zip(chunks, terms)]
                 return (gacc + (sums[0] if len(sums) == 1 else jnp.concatenate(sums, axis=1))) / MICRO_STEPS
 
             return add
 
         def finish(chunks, gacc):
-            return chain.step(grads_of(chunks), ([chunk.terms for chunk in chunks], gacc))
-
-        up_one[0].next()
-        up_one[1].next()
+            return chain.step(grads_of(chunks, gacc), [chunk.terms for chunk in chunks])
+
         grad_down_two = finish([down_two], gacc_down[1])
-        grad_up_two = finish(up_two, gacc_up[1])
-        grad_down_one = finish(down_one, gacc_down[0])
-        up_one[2].next()
-        up_one[3].next()
-        grad_up_one = finish(up_one, gacc_up[0])
+        grad_up_two = finish([up_two], gacc_up[1])
+        up_one_right.far()
+        grad_down_one = finish([down_one], gacc_down[0])
+        grad_up_one = finish([up_one_left, up_one_right], gacc_up[0])
 
         grads = (grad_up_one, grad_down_one, grad_up_two, grad_down_two)
         local_sq = chain.step(lambda v: sum(jnp.sum(g * g) for g in v), grads)
         clip_factor = jnp.minimum(1.0, clip_norm / jnp.sqrt(total_square(local_sq, place)))
         chain.last = None
         new_up = chain.step(lambda v: adamw_update(*v[:3], jnp.stack(v[3:5]) * v[5]), (master_up, mom1_up, mom2_up, grad_up_one, grad_up_two, clip_factor))
-        where = jnp.stack([place.at[d] for d in "zyxc"]).astype(jnp.int32)
-        up_a, up_b = [Gather(place, where, new_up[0][i].astype(BF16)) for i in (0, 1)]
-        up_a.send_z()
+        up_shards = [new_up[0][i].astype(BF16) for i in (0, 1)]
+        half_ff = ff_width // 2
+        up_left, up_right = Gather(place, where, up_shards[0][:, :half_ff]), Gather(place, where, up_shards[0][:, half_ff:])
+        up_b = Gather(place, where, up_shards[1])
+        up_left.send_z()
+        up_right.send_z()
         new_down = chain.step(lambda v: adamw_update(*v[:3], jnp.stack(v[3:5]) * v[5]), (master_down, mom1_down, mom2_down, grad_down_one, grad_down_two, clip_factor))
         down_a, down_b = [Gather(place, where, new_down[0][i].astype(BF16)) for i in (0, 1)]
+        up_left.send_second()
         down_a.send_z()
-        up_b.send_z()
-        up_a.send_second()
-        down_b.send_z()
-        up_a.send_third()
+        up_right.send_second()
+        up_left.send_third()
+        up_right.send_third()
+        up_left.send_core()
         down_a.send_second()
-        up_a.send_core()
-        down_a.send_third()
-        up_b.send_second()
-
-        def up_mul(values):
-            return gelu_fn(dot(values[0], values[1], 1, 0)).astype(BF16)
 
         def down_mul(values):
             return (values[0].astype(F32) + dot(values[1], values[2], 1, 0)).astype(BF16)
 
         hidden_state = x_next.reshape(-1, model_width)
-        act = chain.step(up_mul, (hidden_state, up_a.whole()))
+        weight = up_left.whole()
+        down_a.send_third()
+        up_b.send_z()
+        act = chain.step(lambda v: hidden_act(*v, part=0, n_parts=2), (hidden_state, weight))
+        up_right.send_core()
+        weight = up_right.whole()
         down_a.send_core()
+        up_b.send_second()
+        act = chain.step(lambda v: hidden_act(*v[:2], part=1, n_parts=2, act=v[2]), (hidden_state, weight, act))
+        down_b.send_z()
         up_b.send_third()
+        hidden_state = chain.step(down_mul, (hidden_state, act, down_a.whole()))
         down_b.send_second()
-        hidden_state = chain.step(down_mul, (hidden_state, act, down_a.whole()))
         up_b.send_core()
+        weight = up_b.whole()
         down_b.send_third()
-        act = chain.step(up_mul, (hidden_state, up_b.whole()))
+        act = chain.step(lambda v: hidden_act(*v), (hidden_state, weight))
         down_b.send_core()
         hidden_state = chain.step(down_mul, (hidden_state, act, down_b.whole()))
         return (hidden_state.reshape(x_next.shape), new_up[0], new_down[0], new_up[1], new_down[1], new_up[2], new_down[2])

time: 1370 us -> 1160 us (0.85)
  starting transfers between devices: 245 us -> 141 us
  Pallas kernels: 187 us -> 266 us
  local copies, waits for them, and re-layouts: 114 us -> 37.3 us
  matrix products: 256 us -> 195 us
  waiting for transfers between devices: 490 us -> 437 us
    ppermute x130 -> x112, starting transfers between devices: 245 us -> 141 us  [swap(): lax.ppermute(value, 'fsdp', [(i, i ^ mask) for i in range(self.n_dev)])]
    pallas_call x0 -> x6, Pallas kernels: none -> 89.4 us  [the longest x3 58.2 us: hidden_act(): pl.pallas_call(functools.partial(act_kernel, 6), grid=(steps,), in_specs=...]
    dot_general x10 -> x8, matrix products: 256 us -> 195 us  [dot(): lax.dot_general(lhs, rhs, (((lhs_dim,), (rhs_dim,)), ((), ())), preferred...]
    ppermute x130 -> x112, waiting for transfers between devices: 490 us -> 437 us  [swap(): lax.ppermute(value, 'fsdp', [(i, i ^ mask) for i in range(self.n_dev)])]
    dynamic_slice x33 -> x0, local copies, waits for them, and re-layouts: 30.4 us -> none  [block(): piece = lax.dynamic_slice(part, starts, sizes)]
    squeeze x69 -> x5, local copies, waits for them, and re-layouts: 27.8 us -> 0.45 us  [pick(): return lax.dynamic_index_in_dim(value, index, axis, keepdims=False)]
    squeeze x4 -> x0, local copies, waits for them, and re-layouts: 21.9 us -> none  [the longest x1 12.8 us: run(): w_up[1]]
    pallas_call x8 -> x10, Pallas kernels: 70.4 us -> 61 us  [join(): pl.pallas_call(functools.partial(join_kernel, last), grid_spec=pltpu.Pref...]
  transfers between devices with their start and end apart: 130 -> 112, of which waited for: 53 -> 41; matrix products, arithmetic and copies ran while one was open for 26% -> 19% of each run, Pallas kernels for 10% -> 19%
where the time goes in v2:
time: 1160 us; the launch traced here: 1150 us
  waiting for transfers between devices  437 us (38%)
  Pallas kernels  266 us (23%)
  matrix products  195 us (17%)
  starting transfers between devices  141 us (12%)
  other arithmetic  60.5 us (5%)
  local copies, waits for them, and re-layouts  37.3 us (3%)
    ppermute x112, waiting for transfers between devices, swap(): lax.ppermute(value, 'fsdp', [(i, i ^ mask) for i in range(self.n_dev)])  437 us
    dot_general x8, matrix products, dot(): lax.dot_general(lhs, rhs, (((lhs_dim,), (rhs_dim,)), ((), ())), preferred...  195 us
    ppermute x112, starting transfers between devices, swap(): lax.ppermute(value, 'fsdp', [(i, i ^ mask) for i in range(self.n_dev)])  141 us
    pallas_call x3, Pallas kernels, hidden_pair(): pl.pallas_call(kernel, grid=(steps,), in_specs=in_specs, out_specs=[pl.Bl...  116 us
    pallas_call x10, Pallas kernels, join(): pl.pallas_call(functools.partial(join_kernel, last), grid_spec=pltpu.Pref...  61 us
    pallas_call x3, Pallas kernels, hidden_act(): pl.pallas_call(functools.partial(act_kernel, 6), grid=(steps,), in_specs=...  58.2 us
    pallas_call x3, Pallas kernels, pack(): pl.pallas_call(functools.partial(pack_kernel, orders, width), grid_spec=p...  31.2 us
    add x20, other arithmetic, total(): picked = [sum(picked[i:i + 2]) for i in range(0, len(picked), 2)]  31.2 us
  transfers between devices with their start and end apart: 112, of which 41 were waited for; matrix products, arithmetic and copies ran while one was open for 19% of the time, Pallas kernels for 19%

profile of v2, /device:TPU:0, one launch (start us, length us, event | category | flops | bytes accessed | tf_op | source)
XLA Modules:
  0.0 1146.4 jit_solution(2274706135180726331)
XLA Ops:
  0.7 30.3 %shard_map.180 = (bf16[1536,2560]{1,0:T(8,128)(2,1)}, bf16[1536,5120]{1,0:T(8,128)(2,1)}) custom-call(bf16[2,1536,1280]{2,1,0:T(8,128)(2,1)} %bitcast.308, bf16[1536,1280]{1,0:T(8,128)(2,1)} %bitcast.322, bf16[2,1280,5120]{2,1,0:T(8,128)(2,1)} %up_ref.3, bf16[2,5120,1280]{2,1,0:T(8,128)(2,1)} %down_ref.3), custom_call_target="tpu_custom_call" | custom-call | flops 20132659200 | bytes 35000000 | tf_op jit(solution)/shard_map/pallas_call | solution.py:306
  31.0 14.5 %convolution_convert_fusion.4 = bf16[2560,1280]{1,0:T(8,128)(2,1)} fusion(bf16[1536,2560]{1,0:T(8,128)(2,1)} %get-tuple-element.275, bf16[1,1536,1280]{2,1,0:T(8,128)(2,1)S(1)} %copy-done.10), kind=kOutput, calls=%fused_computation.7 | convolution fusion | flops 10069606400 | bytes 18350080 | tf_op jit(solution)/shard_map/dot_general | solution.py:38
  55.1 31.0 %shard_map.181 = (bf16[1536,2560]{1,0:T(8,128)(2,1)}, bf16[1536,5120]{1,0:T(8,128)(2,1)}) custom-call(bf16[2,1536,1280]{2,1,0:T(8,128)(2,1)} %bitcast.309, bf16[1536,1280]{1,0:T(8,128)(2,1)} %bitcast.323, bf16[2,1280,5120]{2,1,0:T(8,128)(2,1)} %up_ref.3, bf16[2,5120,1280]{2,1,0:T(8,128)(2,1)} %down_ref.3, ...), custom_call_target="tpu_custom_call", output_to_operand_aliasing={{1}: (4, {})} | custom-call | flops 20132659200 | bytes 35000000 | tf_op jit(solution)/shard_map/pallas_call | solution.py:306
  86.1 14.4 %convolution_convert_fusion.3 = bf16[2560,1280]{1,0:T(8,128)(2,1)} fusion(bf16[1536,2560]{1,0:T(8,128)(2,1)} %get-tuple-element.283, bf16[1,1536,1280]{2,1,0:T(8,128)(2,1)S(1)} %copy-done.11), kind=kOutput, calls=%fused_computation.6 | convolution fusion | flops 10069606400 | bytes 18350080 | tf_op jit(solution)/shard_map/dot_general | solution.py:38
  108.7 26.4 %convolution_convert_fusion.2 = bf16[5120,1280]{0,1:T(8,128)(2,1)} fusion(bf16[1536,5120]{1,0:T(8,128)(2,1)S(1)} %copy-done.3, bf16[2,1,1536,1280]{3,2,1,0:T(8,128)(2,1)} %param.13), kind=kOutput, calls=%fused_computation.2 | convolution fusion | flops 20139212800 | bytes 32768000 | tf_op jit(solution)/shard_map/dot_general | solution.py:38
  137.0 10.2 pack.3
  158.8 28.4 %fusion.6.g_ref = bf16[1536,1280]{1,0:T(8,128)(2,1)} fusion(bf16[1536,5120]{1,0:T(8,128)(2,1)} %get-tuple-element.300, bf16[2,1280,5120]{2,1,0:T(8,128)(2,1)} %up_ref.3, bf16[1,1536,1280]{2,1,0:T(8,128)(2,1)} %param.14), kind=kOutput, calls=%fused_computation.11 | convolution fusion | flops 20138557440 | bytes 36700160 | tf_op jit(solution)/shard_map/dot_general | solution.py:38
  197.1 54.8 %shard_map.182 = (bf16[1536,5120]{1,0:T(8,128)(2,1)}, bf16[1536,5120]{1,0:T(8,128)(2,1)}) custom-call(bf16[2,1536,1280]{2,1,0:T(8,128)(2,1)} %bitcast.310, bf16[1536,1280]{1,0:T(8,128)(2,1)} %fusion.6.g_ref, bf16[2,1280,5120]{2,1,0:T(8,128)(2,1)} %up_ref.3, bf16[2,5120,1280]{2,1,0:T(8,128)(2,1)} %down_ref.3), custom_call_target="tpu_custom_call" | custom-call | flops 40265318400 | bytes 70000000 | tf_op jit(solution)/shard_map/pallas_call | solution.py:306
  253.9 9.3 collective-permute-done.13
  277.2 27.8 %convolution_convert_fusion.1 = bf16[5120,1280]{1,0:T(8,128)(2,1)} fusion(bf16[1536,5120]{1,0:T(8,128)(2,1)S(1)} %copy-done.74, bf16[1536,1280]{1,0:T(8,128)(2,1)} %fusion.6.g_ref), kind=kOutput, calls=%fused_computation.1 | convolution fusion | flops 20139212800 | bytes 32768000 | tf_op jit(solution)/shard_map/dot_general | solution.py:38
  304.9 10.5 pack.4
  321.6 26.4 %convolution_convert_fusion = bf16[5120,1280]{0,1:T(8,128)(2,1)} fusion(bf16[1536,5120]{1,0:T(8,128)(2,1)} %get-tuple-element.334, bf16[2,1,1536,1280]{3,2,1,0:T(8,128)(2,1)} %param.13), kind=kOutput, calls=%fused_computation | convolution fusion | flops 20139212800 | bytes 32768000 | tf_op jit(solution)/shard_map/dot_general | solution.py:38
  348.0 10.6 pack.5
  369.0 31.3 %collective-permute-done.25 = bf16[2,4,160,640]{3,2,1,0:T(8,128)(2,1)S(1)} collective-permute-done((bf16[2,4,160,640]{3,2,1,0:T(8,128)(2,1)S(1)}, bf16[2,4,160,640]{3,2,1,0:T(8,128)(2,1)S(1)}, u32[]{:S(2)}, u32[]{:S(2)}) %collective-permute-start.25) | collective-permute-done | bytes 1638432 | tf_op jit(solution)/shard_map/ppermute | solution.py:67
  401.9 32.7 %collective-permute-done.26 = bf16[2,4,160,640]{3,2,1,0:T(8,128)(2,1)S(1)} collective-permute-done((bf16[2,4,160,640]{3,2,1,0:T(8,128)(2,1)S(1)}, bf16[2,4,160,640]{3,2,1,0:T(8,128)(2,1)S(1)}, u32[]{:S(2)}, u32[]{:S(2)}) %collective-permute-start.26) | collective-permute-done | bytes 1638432 | tf_op jit(solution)/shard_map/ppermute | solution.py:67
  442.2 10.8 collective-permute-done.15
  453.6 16.2 %collective-permute-done.16 = bf16[2,4,40,1280]{3,2,1,0:T(8,128)(2,1)S(1)} collective-permute-done((bf16[2,4,40,1280]{3,2,1,0:T(8,128)(2,1)S(1)}, bf16[2,4,40,1280]{3,2,1,0:T(8,128)(2,1)S(1)}, u32[]{:S(2)}, u32[]{:S(2)}) %collective-permute-start.16) | collective-permute-done | bytes 819232 | tf_op jit(solution)/shard_map/ppermute | solution.py:67
  473.0 20.5 %collective-permute-done.29 = bf16[2,4,40,1280]{3,2,1,0:T(8,128)(2,1)S(1)} collective-permute-done((bf16[2,4,40,1280]{3,2,1,0:T(8,128)(2,1)S(1)}, bf16[2,4,40,1280]{3,2,1,0:T(8,128)(2,1)S(1)}, u32[]{:S(2)}, u32[]{:S(2)}) %collective-permute-start.29) | collective-permute-done | bytes 819232 | tf_op jit(solution)/shard_map/ppermute | solution.py:67
  493.5 15.6 %collective-permute-done.30 = bf16[2,4,40,1280]{3,2,1,0:T(8,128)(2,1)S(1)} collective-permute-done((bf16[2,4,40,1280]{3,2,1,0:T(8,128)(2,1)S(1)}, bf16[2,4,40,1280]{3,2,1,0:T(8,128)(2,1)S(1)}, u32[]{:S(2)}, u32[]{:S(2)}) %collective-permute-start.30) | collective-permute-done | bytes 819232 | tf_op jit(solution)/shard_map/ppermute | solution.py:67
  513.1 14.4 %collective-permute-done.27 = f32[4,40,1280]{2,1,0:T(8,128)S(1)} collective-permute-done((f32[4,40,1280]{2,1,0:T(8,128)S(1)}, f32[4,40,1280]{2,1,0:T(8,128)S(1)}, u32[]{:S(2)}, u32[]{:S(2)}) %collective-permute-start.27) | collective-permute-done | bytes 819232 | tf_op jit(solution)/shard_map/ppermute | solution.py:67
  533.5 15.4 %collective-permute-done.35 = f32[2,160,1280]{2,1,0:T(8,128)S(1)} collective-permute-done((f32[2,160,1280]{2,1,0:T(8,128)S(1)}, f32[2,160,1280]{2,1,0:T(8,128)S(1)}, u32[]{:S(2)}, u32[]{:S(2)}) %collective-permute-start.35) | collective-permute-done | bytes 1638432 | tf_op jit(solution)/shard_map/ppermute | solution.py:67
  552.1 14.3 %collective-permute-done.34 = f32[2,40,2560]{2,1,0:T(8,128)S(1)} collective-permute-done((f32[2,40,2560]{2,1,0:T(8,128)S(1)}, f32[2,40,2560]{2,1,0:T(8,128)S(1)}, u32[]{:S(2)}, u32[]{:S(2)}) %collective-permute-start.34) | collective-permute-done | bytes 819232 | tf_op jit(solution)/shard_map/ppermute | solution.py:67
  572.4 15.9 %collective-permute-done.43 = bf16[2,4,40,1280]{3,2,1,0:T(8,128)(2,1)S(1)} collective-permute-done((bf16[2,4,40,1280]{3,2,1,0:T(8,128)(2,1)S(1)}, bf16[2,4,40,1280]{3,2,1,0:T(8,128)(2,1)S(1)}, u32[]{:S(2)}, u32[]{:S(2)}) %collective-permute-start.43) | collective-permute-done | bytes 819232 | tf_op jit(solution)/shard_map/ppermute | solution.py:67
  595.8 10.7 collective-permute-done.40
  611.0 62.6 %collective-permute-done.47 = f32[160,1280]{1,0:T(8,128)S(1)} collective-permute-done((f32[160,1280]{1,0:T(8,128)S(1)}, f32[160,1280]{1,0:T(8,128)S(1)}, u32[]{:S(2)}, u32[]{:S(2)}) %collective-permute-start.47) | collective-permute-done | bytes 819232 | tf_op jit(solution)/shard_map/ppermute | solution.py:67
  673.7 17.4 %collective-permute-done.46 = f32[40,5120]{1,0:T(8,128)S(1)} collective-permute-done((f32[40,5120]{1,0:T(8,128)S(1)}, f32[40,5120]{1,0:T(8,128)S(1)}, u32[]{:S(2)}, u32[]{:S(2)}) %collective-permute-start.46) | collective-permute-done | bytes 819232 | tf_op jit(solution)/shard_map/ppermute | solution.py:67
  691.5 34.7 %collective-permute-done.49 = f32[160,1280]{1,0:T(8,128)S(1)} collective-permute-done((f32[160,1280]{1,0:T(8,128)S(1)}, f32[160,1280]{1,0:T(8,128)S(1)}, u32[]{:S(2)}, u32[]{:S(2)}) %collective-permute-start.49) | collective-permute-done | bytes 819232 | tf_op jit(solution)/shard_map/ppermute | solution.py:67
  726.4 8.6 collective-permute-done.48
  789.2 10.9 collective-permute-done.61
  804.9 7.8 collective-permute-done.65
  820.5 7.0 collective-permute-start.76
  834.7 12.2 %collective-permute-done.76 = bf16[160,1280]{1,0:T(8,128)(2,1)S(1)} collective-permute-done((bf16[160,1280]{1,0:T(8,128)(2,1)S(1)}, bf16[160,1280]{1,0:T(8,128)(2,1)S(1)}, u32[]{:S(2)}, u32[]{:S(2)}) %collective-permute-start.76) | collective-permute-done | bytes 409632 | tf_op jit(solution)/shard_map/ppermute | solution.py:67
  862.8 5.7 collective-permute-done.78
  876.4 15.2 %shard_map.185.refs_0_ = bf16[1536,5120]{1,0:T(8,128)(2,1)} custom-call(bf16[1536,1280]{1,0:T(8,128)(2,1)S(1)} %bitcast.298, bf16[1280,2560]{1,0:T(8,128)(2,1)} %bitcast.304), custom_call_target="tpu_custom_call" | custom-call | flops 10066329600 | bytes 16500000 | tf_op jit(solution)/shard_map/pallas_call | solution.py:340
  913.6 8.2 collective-permute-done.87.far
  921.8 8.8 collective-permute-done.85
  935.3 15.3 %collective-permute-done.93 = bf16[4,40,2560]{2,1,0:T(8,128)(2,1)S(1)} collective-permute-done((bf16[4,40,2560]{2,1,0:T(8,128)(2,1)S(1)}, bf16[4,40,2560]{2,1,0:T(8,128)(2,1)S(1)}, u32[]{:S(2)}, u32[]{:S(2)}) %collective-permute-start.93) | collective-permute-done | bytes 819232 | tf_op jit(solution)/shard_map/ppermute | solution.py:67
  952.1 15.3 %shard_map.188 = bf16[1536,5120]{1,0:T(8,128)(2,1)} custom-call(bf16[1536,1280]{1,0:T(8,128)(2,1)S(1)} %bitcast.299, bf16[1280,2560]{1,0:T(8,128)(2,1)} %bitcast.300, bf16[1536,5120]{1,0:T(8,128)(2,1)} %shard_map.185.refs_0_), custom_call_target="tpu_custom_call", output_to_operand_aliasing={{}: (2, {})} | custom-call | flops 10066329600 | bytes 16500000 | tf_op jit(solution)/shard_map/pallas_call | solution.py:340
  967.4 11.5 collective-permute-start.97
  989.8 6.8 shard_map.189.refs_0_
  996.6 6.8 shard_map.190
  1003.4 28.1 %fusion.9.x_ref = bf16[1536,1280]{1,0:T(8,128)(2,1)} fusion(bf16[1536,5120]{1,0:T(8,128)(2,1)} %shard_map.188, bf16[5120,1280]{1,0:T(8,128)(2,1)} %bitcast.302, bf16[1536,1280]{1,0:T(8,128)(2,1)} %bitcast.297), kind=kOutput, calls=%fused_computation.12 | convolution fusion | flops 20138557440 | bytes 36700160 | tf_op jit(solution)/shard_map/dot_general | solution.py:38
  1042.2 6.7 shard_map.191.refs_0_
  1048.9 6.7 shard_map.192
  1063.0 27.7 %shard_map.193 = bf16[1536,5120]{1,0:T(8,128)(2,1)} custom-call(bf16[1536,1280]{1,0:T(8,128)(2,1)S(1)} %copy-done.2, bf16[1280,5120]{1,0:T(8,128)(2,1)} %bitcast.303), custom_call_target="tpu_custom_call" | custom-call | flops 20132659200 | bytes 33000000 | tf_op jit(solution)/shard_map/pallas_call | solution.py:340
  1104.0 6.8 shard_map.194.refs_0_
  1110.8 6.8 shard_map.195
  1117.6 28.4 %fusion.11 = bf16[1,1536,1280]{2,1,0:T(8,128)(2,1)} fusion(bf16[1536,5120]{1,0:T(8,128)(2,1)} %shard_map.193, bf16[5120,1280]{1,0:T(8,128)(2,1)} %bitcast.301, bf16[1536,1280]{1,0:T(8,128)(2,1)} %fusion.9.x_ref), kind=kOutput, calls=%fused_computation.14 | convolution fusion | flops 20138557440 | bytes 36700160 | tf_op jit(solution)/shard_map/dot_general | solution.py:38
  (454 shorter events, 278.8 us)
Async XLA Ops:
  49.4 102.0 %collective-permute-start = (bf16[2,2,160,1280]{3,2,1,0:T(8,128)(2,1)}, bf16[2,2,160,1280]{3,2,1,0:T(8,128)(2,1)S(1)}, u32[]{:S(2)}, u32[]{:S(2)}) collective-permute-start(bf16[2,2,160,1280]{3,2,1,0:T(8,128)(2,1)} %get-tuple-element.562), channel_id=1, source_target_pairs={{0,1},{1,0},{2,3},{3,2},{4,5},{5,4},{6,7},{7,6},{8,9},{9,8},{10,11... | collective-permute-start | bytes 4915208 | tf_op jit(solution)/shard_map/ppermute | solution.py:67
  51.2 101.9 %collective-permute-start.1 = (bf16[2,2,160,1280]{3,2,0,1:T(8,128)(2,1)}, bf16[2,2,160,1280]{3,2,0,1:T(8,128)(2,1)}, u32[]{:S(2)}, u32[]{:S(2)}) collective-permute-start(bf16[2,2,160,1280]{3,2,0,1:T(8,128)(2,1)} %copy.31), channel_id=1, source_target_pairs={{0,2},{1,3},{2,0},{3,1},{4,6},{5,7},{6,4},{7,5},{8,10},{9,11},{10,... | collective-permute-start | bytes 4915208 | tf_op jit(solution)/shard_map/ppermute | solution.py:67
  54.9 98.4 %collective-permute-start.2 = (bf16[2,2,160,1280]{3,2,0,1:T(8,128)(2,1)}, bf16[2,2,160,1280]{3,2,0,1:T(8,128)(2,1)}, u32[]{:S(2)}, u32[]{:S(2)}) collective-permute-start(bf16[2,2,160,1280]{3,2,0,1:T(8,128)(2,1)} %copy.32), channel_id=1, source_target_pairs={{0,3},{1,2},{2,1},{3,0},{4,7},{5,6},{6,5},{7,4},{8,11},{9,10},{10,... | collective-permute-start | bytes 4915208 | tf_op jit(solution)/shard_map/ppermute | solution.py:67
  104.7 82.5 %collective-permute-start.3 = (bf16[2,2,160,1280]{3,2,0,1:T(8,128)(2,1)}, bf16[2,2,160,1280]{3,2,0,1:T(8,128)(2,1)}, u32[]{:S(2)}, u32[]{:S(2)}) collective-permute-start(bf16[2,2,160,1280]{3,2,0,1:T(8,128)(2,1)} %copy.40), channel_id=1, source_target_pairs={{0,1},{1,0},{2,3},{3,2},{4,5},{5,4},{6,7},{7,6},{8,9},{9,8},{10,11... | collective-permute-start | bytes 4915208 | tf_op jit(solution)/shard_map/ppermute | solution.py:67
  106.1 82.0 %collective-permute-start.4 = (bf16[2,2,160,1280]{3,2,0,1:T(8,128)(2,1)}, bf16[2,2,160,1280]{3,2,0,1:T(8,128)(2,1)}, u32[]{:S(2)}, u32[]{:S(2)}) collective-permute-start(bf16[2,2,160,1280]{3,2,0,1:T(8,128)(2,1)} %copy.41), channel_id=1, source_target_pairs={{0,4},{1,5},{2,6},{3,7},{4,0},{5,1},{6,2},{7,3},{8,12},{9,13},{10,... | collective-permute-start | bytes 4915208 | tf_op jit(solution)/shard_map/ppermute | solution.py:67
  153.1 116.9 %collective-permute-start.8 = (bf16[2,4,40,2560]{3,2,1,0:T(8,128)(2,1)}, bf16[2,4,40,2560]{3,2,1,0:T(8,128)(2,1)}, u32[]{:S(2)}, u32[]{:S(2)}) collective-permute-start(bf16[2,4,40,2560]{3,2,1,0:T(8,128)(2,1)} %get-tuple-element.293), channel_id=1, source_target_pairs={{0,1},{1,0},{2,3},{3,2},{4,5},{5,4},{6,7},{7,6},{8,9},{9,8},{10,11... | collective-permute-start | bytes 4915208 | tf_op jit(solution)/shard_map/ppermute | solution.py:67
  153.3 43.7 %collective-permute-start.11 = (bf16[2,4,40,2560]{3,2,1,0:T(8,128)(2,1)}, bf16[2,4,40,2560]{3,2,1,0:T(8,128)(2,1)}, u32[]{:S(2)}, u32[]{:S(2)}) collective-permute-start(bf16[2,4,40,2560]{3,2,1,0:T(8,128)(2,1)} %get-tuple-element.289), channel_id=1, source_target_pairs={{0,1},{1,0},{2,3},{3,2},{4,5},{5,4},{6,7},{7,6},{8,9},{9,8},{10,11... | collective-permute-start | bytes 4915208 | tf_op jit(solution)/shard_map/ppermute | solution.py:67
  187.3 85.0 %collective-permute-start.9 = (bf16[2,4,40,2560]{3,2,1,0:T(8,128)(2,1)}, bf16[2,4,40,2560]{3,2,1,0:T(8,128)(2,1)S(1)}, u32[]{:S(2)}, u32[]{:S(2)}) collective-permute-start(bf16[2,4,40,2560]{3,2,1,0:T(8,128)(2,1)} %get-tuple-element.294), channel_id=1, source_target_pairs={{0,4},{1,5},{2,6},{3,7},{4,0},{5,1},{6,2},{7,3},{8,12},{9,13},{10,... | collective-permute-start | bytes 4915208 | tf_op jit(solution)/shard_map/ppermute | solution.py:67
  188.1 84.2 %collective-permute-start.10 = (bf16[2,4,40,2560]{3,2,1,0:T(8,128)(2,1)}, bf16[2,4,40,2560]{3,2,1,0:T(8,128)(2,1)}, u32[]{:S(2)}, u32[]{:S(2)}) collective-permute-start(bf16[2,4,40,2560]{3,2,1,0:T(8,128)(2,1)} %get-tuple-element.295), channel_id=1, source_target_pairs={{0,5},{1,4},{2,7},{3,6},{4,1},{5,0},{6,3},{7,2},{8,13},{9,12},{10,... | collective-permute-start | bytes 4915208 | tf_op jit(solution)/shard_map/ppermute | solution.py:67
  190.7 61.1 %collective-permute-start.12 = (bf16[2,4,40,2560]{3,2,1,0:T(8,128)(2,1)}, bf16[2,4,40,2560]{3,2,1,0:T(8,128)(2,1)}, u32[]{:S(2)}, u32[]{:S(2)}) collective-permute-start(bf16[2,4,40,2560]{3,2,1,0:T(8,128)(2,1)} %get-tuple-element.290), channel_id=1, source_target_pairs={{0,2},{1,3},{2,0},{3,1},{4,6},{5,7},{6,4},{7,5},{8,10},{9,11},{10,... | collective-permute-start | bytes 4915208 | tf_op jit(solution)/shard_map/ppermute | solution.py:67
  197.0 66.1 %collective-permute-start.13 = (bf16[2,4,40,2560]{3,2,1,0:T(8,128)(2,1)}, bf16[2,4,40,2560]{3,2,1,0:T(8,128)(2,1)}, u32[]{:S(2)}, u32[]{:S(2)}) collective-permute-start(bf16[2,4,40,2560]{3,2,1,0:T(8,128)(2,1)} %get-tuple-element.291), channel_id=1, source_target_pairs={{0,3},{1,2},{2,1},{3,0},{4,7},{5,6},{6,5},{7,4},{8,11},{9,10},{10,... | collective-permute-start | bytes 4915208 | tf_op jit(solution)/shard_map/ppermute | solution.py:67
  251.8 63.8 %collective-permute-start.6 = (f32[2,160,1280]{2,1,0:T(8,128)}, f32[2,160,1280]{2,1,0:T(8,128)}, u32[]{:S(2)}, u32[]{:S(2)}) collective-permute-start(f32[2,160,1280]{2,1,0:T(8,128)} %fusion.30), channel_id=1, source_target_pairs={{0,4},{1,5},{2,6},{3,7},{4,0},{5,1},{6,2},{7,3},{8,12},{9,13},{10,... | collective-permute-start | bytes 4915208 | tf_op jit(solution)/shard_map/ppermute | solution.py:67
  263.1 53.1 %collective-permute-start.7 = (f32[2,160,1280]{2,1,0:T(8,128)}, f32[2,160,1280]{2,1,0:T(8,128)}, u32[]{:S(2)}, u32[]{:S(2)}) collective-permute-start(f32[2,160,1280]{2,1,0:T(8,128)} %get-tuple-element.555), channel_id=1, source_target_pairs={{0,2},{1,3},{2,0},{3,1},{4,6},{5,7},{6,4},{7,5},{8,10},{9,11},{10,... | collective-permute-start | bytes 4915208 | tf_op jit(solution)/shard_map/ppermute | solution.py:67
  270.0 89.9 %collective-permute-start.17 = (f32[4,40,2560]{2,1,0:T(8,128)}, f32[4,40,2560]{2,1,0:T(8,128)}, u32[]{:S(2)}, u32[]{:S(2)}) collective-permute-start(f32[4,40,2560]{2,1,0:T(8,128)} %get-tuple-element.553), channel_id=1, source_target_pairs={{0,4},{1,5},{2,6},{3,7},{4,0},{5,1},{6,2},{7,3},{8,12},{9,13},{10,... | collective-permute-start | bytes 4915208 | tf_op jit(solution)/shard_map/ppermute | solution.py:67
  276.9 84.8 %collective-permute-start.18 = (f32[4,40,2560]{2,1,0:T(8,128)}, f32[4,40,2560]{2,1,0:T(8,128)}, u32[]{:S(2)}, u32[]{:S(2)}) collective-permute-start(f32[4,40,2560]{2,1,0:T(8,128)} %get-tuple-element.551), channel_id=1, source_target_pairs={{0,2},{1,3},{2,0},{3,1},{4,6},{5,7},{6,4},{7,5},{8,10},{9,11},{10,... | collective-permute-start | bytes 4915208 | tf_op jit(solution)/shard_map/ppermute | solution.py:67
  315.4 51.5 %collective-permute-start.21 = (bf16[2,4,160,640]{3,2,1,0:T(8,128)(2,1)}, bf16[2,4,160,640]{3,2,1,0:T(8,128)(2,1)}, u32[]{:S(2)}, u32[]{:S(2)}) collective-permute-start(bf16[2,4,160,640]{3,2,1,0:T(8,128)(2,1)} %get-tuple-element.327), channel_id=1, source_target_pairs={{0,1},{1,0},{2,3},{3,2},{4,5},{5,4},{6,7},{7,6},{8,9},{9,8},{10,11... | collective-permute-start | bytes 4915208 | tf_op jit(solution)/shard_map/ppermute | solution.py:67
  315.7 52.3 %collective-permute-start.22 = (bf16[2,4,160,640]{3,2,1,0:T(8,128)(2,1)}, bf16[2,4,160,640]{3,2,1,0:T(8,128)(2,1)}, u32[]{:S(2)}, u32[]{:S(2)}) collective-permute-start(bf16[2,4,160,640]{3,2,1,0:T(8,128)(2,1)} %get-tuple-element.328), channel_id=1, source_target_pairs={{0,4},{1,5},{2,6},{3,7},{4,0},{5,1},{6,2},{7,3},{8,12},{9,13},{10,... | collective-permute-start | bytes 4915208 | tf_op jit(solution)/shard_map/ppermute | solution.py:67
  358.6 78.6 %collective-permute-start.23 = (bf16[2,4,160,640]{3,2,1,0:T(8,128)(2,1)}, bf16[2,4,160,640]{3,2,1,0:T(8,128)(2,1)S(1)}, u32[]{:S(2)}, u32[]{:S(2)}) collective-permute-start(bf16[2,4,160,640]{3,2,1,0:T(8,128)(2,1)} %get-tuple-element.329), channel_id=1, source_target_pairs={{0,5},{1,4},{2,7},{3,6},{4,1},{5,0},{6,3},{7,2},{8,13},{9,12},{10,... | collective-permute-start | bytes 4915208 | tf_op jit(solution)/shard_map/ppermute | solution.py:67
  361.7 38.7 %collective-permute-start.25 = (bf16[2,4,160,640]{3,2,1,0:T(8,128)(2,1)S(1)}, bf16[2,4,160,640]{3,2,1,0:T(8,128)(2,1)S(1)}, u32[]{:S(2)}, u32[]{:S(2)}) collective-permute-start(bf16[2,4,160,640]{3,2,1,0:T(8,128)(2,1)S(1)} %copy-done.60), channel_id=1, source_target_pairs={{0,2},{1,3},{2,0},{3,1},{4,6},{5,7},{6,4},{7,5},{8,10},{9,11},{10,... | collective-permute-start | bytes 4915208 | tf_op jit(solution)/shard_map/ppermute | solution.py:67
  367.1 67.5 %collective-permute-start.26 = (bf16[2,4,160,640]{3,2,1,0:T(8,128)(2,1)S(1)}, bf16[2,4,160,640]{3,2,1,0:T(8,128)(2,1)S(1)}, u32[]{:S(2)}, u32[]{:S(2)}) collective-permute-start(bf16[2,4,160,640]{3,2,1,0:T(8,128)(2,1)S(1)} %copy-done.59), channel_id=1, source_target_pairs={{0,3},{1,2},{2,1},{3,0},{4,7},{5,6},{6,5},{7,4},{8,11},{9,10},{10,... | collective-permute-start | bytes 4915208 | tf_op jit(solution)/shard_map/ppermute | solution.py:67
  368.0 72.5 %collective-permute-start.20 = (f32[2,40,5120]{2,1,0:T(8,128)S(1)}, f32[2,40,5120]{2,1,0:T(8,128)S(1)}, u32[]{:S(2)}, u32[]{:S(2)}) collective-permute-start(f32[2,40,5120]{2,1,0:T(8,128)S(1)} %get-tuple-element.573), channel_id=1, source_target_pairs={{0,8},{1,9},{2,10},{3,11},{4,12},{5,13},{6,14},{7,15},{8,0},{9,1},... | collective-permute-start | bytes 4915208 | tf_op jit(solution)/shard_map/ppermute | solution.py:67
  369.0 72.3 %collective-permute-start.14 = (bf16[2,4,40,1280]{3,2,1,0:T(8,128)(2,1)S(1)}, bf16[2,4,40,1280]{3,2,1,0:T(8,128)(2,1)S(1)}, u32[]{:S(2)}, u32[]{:S(2)}) collective-permute-start(bf16[2,4,40,1280]{3,2,1,0:T(8,128)(2,1)S(1)} %copy-done.73), channel_id=1, source_target_pairs={{0,1},{1,0},{2,3},{3,2},{4,5},{5,4},{6,7},{7,6},{8,9},{9,8},{10,11... | collective-permute-start | bytes 2457608 | tf_op jit(solution)/shard_map/ppermute | solution.py:67
  400.4 52.7 %collective-permute-start.15 = (bf16[2,4,40,1280]{3,2,1,0:T(8,128)(2,1)S(1)}, bf16[2,4,40,1280]{3,2,1,0:T(8,128)(2,1)S(1)}, u32[]{:S(2)}, u32[]{:S(2)}) collective-permute-start(bf16[2,4,40,1280]{3,2,1,0:T(8,128)(2,1)S(1)} %copy-done.72), channel_id=1, source_target_pairs={{0,2},{1,3},{2,0},{3,1},{4,6},{5,7},{6,4},{7,5},{8,10},{9,11},{10,... | collective-permute-start | bytes 2457608 | tf_op jit(solution)/shard_map/ppermute | solution.py:67
  437.2 72.8 %collective-permute-start.32 = (f32[4,160,640]{2,1,0:T(8,128)S(1)}, f32[4,160,640]{2,1,0:T(8,128)S(1)}, u32[]{:S(2)}, u32[]{:S(2)}) collective-permute-start(f32[4,160,640]{2,1,0:T(8,128)S(1)} %get-tuple-element.549), channel_id=1, source_target_pairs={{0,4},{1,5},{2,6},{3,7},{4,0},{5,1},{6,2},{7,3},{8,12},{9,13},{10,... | collective-permute-start | bytes 4915208 | tf_op jit(solution)/shard_map/ppermute | solution.py:67
  440.5 69.5 %collective-permute-start.33 = (f32[4,160,640]{2,1,0:T(8,128)S(1)}, f32[4,160,640]{2,1,0:T(8,128)S(1)}, u32[]{:S(2)}, u32[]{:S(2)}) collective-permute-start(f32[4,160,640]{2,1,0:T(8,128)S(1)} %get-tuple-element.547), channel_id=1, source_target_pairs={{0,2},{1,3},{2,0},{3,1},{4,6},{5,7},{6,4},{7,5},{8,10},{9,11},{10,... | collective-permute-start | bytes 4915208 | tf_op jit(solution)/shard_map/ppermute | solution.py:67
  453.1 40.4 %collective-permute-start.29 = (bf16[2,4,40,1280]{3,2,1,0:T(8,128)(2,1)S(1)}, bf16[2,4,40,1280]{3,2,1,0:T(8,128)(2,1)S(1)}, u32[]{:S(2)}, u32[]{:S(2)}) collective-permute-start(bf16[2,4,40,1280]{3,2,1,0:T(8,128)(2,1)S(1)} %copy-done.69), channel_id=1, source_target_pairs={{0,4},{1,5},{2,6},{3,7},{4,0},{5,1},{6,2},{7,3},{8,12},{9,13},{10,... | collective-permute-start | bytes 2457608 | tf_op jit(solution)/shard_map/ppermute | solution.py:67
  469.7 39.3 %collective-permute-start.30 = (bf16[2,4,40,1280]{3,2,1,0:T(8,128)(2,1)S(1)}, bf16[2,4,40,1280]{3,2,1,0:T(8,128)(2,1)S(1)}, u32[]{:S(2)}, u32[]{:S(2)}) collective-permute-start(bf16[2,4,40,1280]{3,2,1,0:T(8,128)(2,1)S(1)} %copy-done.68), channel_id=1, source_target_pairs={{0,5},{1,4},{2,7},{3,6},{4,1},{5,0},{6,3},{7,2},{8,13},{9,12},{10,... | collective-permute-start | bytes 2457608 | tf_op jit(solution)/shard_map/ppermute | solution.py:67
  471.4 56.1 %collective-permute-start.27 = (f32[4,40,1280]{2,1,0:T(8,128)S(1)}, f32[4,40,1280]{2,1,0:T(8,128)S(1)}, u32[]{:S(2)}, u32[]{:S(2)}) collective-permute-start(f32[4,40,1280]{2,1,0:T(8,128)S(1)} %get-tuple-element.571), channel_id=1, source_target_pairs={{0,4},{1,5},{2,6},{3,7},{4,0},{5,1},{6,2},{7,3},{8,12},{9,13},{10,... | collective-permute-start | bytes 2457608 | tf_op jit(solution)/shard_map/ppermute | solution.py:67
  590.3 83.3 %collective-permute-start.47 = (f32[160,1280]{1,0:T(8,128)S(1)}, f32[160,1280]{1,0:T(8,128)S(1)}, u32[]{:S(2)}, u32[]{:S(2)}) collective-permute-start(f32[160,1280]{1,0:T(8,128)S(1)} %get-tuple-element.585), channel_id=1, source_target_pairs={{0,16},{1,17},{2,18},{3,19},{4,20},{5,21},{6,22},{7,23},{8,24},{9,... | collective-permute-start | bytes 2457608 | tf_op jit(solution)/shard_map/ppermute | solution.py:67
  592.9 98.2 %collective-permute-start.46 = (f32[40,5120]{1,0:T(8,128)S(1)}, f32[40,5120]{1,0:T(8,128)S(1)}, u32[]{:S(2)}, u32[]{:S(2)}) collective-permute-start(f32[40,5120]{1,0:T(8,128)S(1)} %get-tuple-element.583), channel_id=1, source_target_pairs={{0,16},{1,17},{2,18},{3,19},{4,20},{5,21},{6,22},{7,23},{8,24},{9,... | collective-permute-start | bytes 2457608 | tf_op jit(solution)/shard_map/ppermute | solution.py:67
  593.2 133.2 %collective-permute-start.36 = (f32[40,2560]{1,0:T(8,128)S(1)}, f32[40,2560]{1,0:T(8,128)S(1)}, u32[]{:S(2)}, u32[]{:S(2)}) collective-permute-start(f32[40,2560]{1,0:T(8,128)S(1)} %get-tuple-element.593), channel_id=1, source_target_pairs={{0,16},{1,17},{2,18},{3,19},{4,20},{5,21},{6,22},{7,23},{8,24},{9,... | collective-permute-start | bytes 1228808 | tf_op jit(solution)/shard_map/ppermute | solution.py:67
  606.5 119.7 %collective-permute-start.49 = (f32[160,1280]{1,0:T(8,128)S(1)}, f32[160,1280]{1,0:T(8,128)S(1)}, u32[]{:S(2)}, u32[]{:S(2)}) collective-permute-start(f32[160,1280]{1,0:T(8,128)S(1)} %get-tuple-element.579), channel_id=1, source_target_pairs={{0,16},{1,17},{2,18},{3,19},{4,20},{5,21},{6,22},{7,23},{8,24},{9,... | collective-permute-start | bytes 2457608 | tf_op jit(solution)/shard_map/ppermute | solution.py:67
  609.9 81.4 %collective-permute-start.45 = (f32[2,40,2560]{2,1,0:T(8,128)S(1)}, f32[2,40,2560]{2,1,0:T(8,128)S(1)}, u32[]{:S(2)}, u32[]{:S(2)}) collective-permute-start(f32[2,40,2560]{2,1,0:T(8,128)S(1)} %get-tuple-element.577), channel_id=1, source_target_pairs={{0,8},{1,9},{2,10},{3,11},{4,12},{5,13},{6,14},{7,15},{8,0},{9,1},... | collective-permute-start | bytes 2457608 | tf_op jit(solution)/shard_map/ppermute | solution.py:67
  691.5 43.5 %collective-permute-start.48 = (f32[40,2560]{1,0:T(8,128)S(1)}, f32[40,2560]{1,0:T(8,128)S(1)}, u32[]{:S(2)}, u32[]{:S(2)}) collective-permute-start(f32[40,2560]{1,0:T(8,128)S(1)} %get-tuple-element.591), channel_id=1, source_target_pairs={{0,16},{1,17},{2,18},{3,19},{4,20},{5,21},{6,22},{7,23},{8,24},{9,... | collective-permute-start | bytes 1228808 | tf_op jit(solution)/shard_map/ppermute | solution.py:67
  848.7 42.8 %collective-permute-start.67 = (bf16[2,4,40,1280]{3,2,1,0:T(8,128)(2,1)S(1)}, bf16[2,4,40,1280]{3,2,1,0:T(8,128)(2,1)}, u32[]{:S(2)}, u32[]{:S(2)}) collective-permute-start(bf16[2,4,40,1280]{3,2,1,0:T(8,128)(2,1)S(1)} %pad_maximum_fusion.8.own), channel_id=1, source_target_pairs={{0,2},{1,3},{2,0},{3,1},{4,6},{5,7},{6,4},{7,5},{8,10},{9,11},{10,... | collective-permute-start | bytes 2457608 | tf_op jit(solution)/shard_map/ppermute | solution.py:67
  850.7 40.8 %collective-permute-start.68 = (bf16[2,4,40,1280]{3,2,1,0:T(8,128)(2,1)}, bf16[2,4,40,1280]{3,2,1,0:T(8,128)(2,1)}, u32[]{:S(2)}, u32[]{:S(2)}) collective-permute-start(bf16[2,4,40,1280]{3,2,1,0:T(8,128)(2,1)} %pad_maximum_fusion.9.own), channel_id=1, source_target_pairs={{0,4},{1,5},{2,6},{3,7},{4,0},{5,1},{6,2},{7,3},{8,12},{9,13},{10,... | collective-permute-start | bytes 2457608 | tf_op jit(solution)/shard_map/ppermute | solution.py:67
  852.6 39.5 %collective-permute-start.80 = (bf16[2,4,40,1280]{3,2,1,0:T(8,128)(2,1)S(1)}, bf16[2,4,40,1280]{3,2,1,0:T(8,128)(2,1)}, u32[]{:S(2)}, u32[]{:S(2)}) collective-permute-start(bf16[2,4,40,1280]{3,2,1,0:T(8,128)(2,1)S(1)} %pad_maximum_fusion.8.own), channel_id=1, source_target_pairs={{0,1},{1,0},{2,3},{3,2},{4,5},{5,4},{6,7},{7,6},{8,9},{9,8},{10,11... | collective-permute-start | bytes 2457608 | tf_op jit(solution)/shard_map/ppermute | solution.py:67
  872.2 49.7 %collective-permute-start.87 = (bf16[2,4,160,640]{3,2,1,0:T(8,128)(2,1)S(1)}, bf16[2,4,160,640]{3,2,1,0:T(8,128)(2,1)}, u32[]{:S(2)}, u32[]{:S(2)}) collective-permute-start(bf16[2,4,160,640]{3,2,1,0:T(8,128)(2,1)S(1)} %pad_maximum_fusion.own), channel_id=1, source_target_pairs={{0,2},{1,3},{2,0},{3,1},{4,6},{5,7},{6,4},{7,5},{8,10},{9,11},{10,... | collective-permute-start | bytes 4915208 | tf_op jit(solution)/shard_map/ppermute | solution.py:67
  875.5 46.3 %collective-permute-start.88 = (bf16[2,4,160,640]{3,2,1,0:T(8,128)(2,1)}, bf16[2,4,160,640]{3,2,1,0:T(8,128)(2,1)}, u32[]{:S(2)}, u32[]{:S(2)}) collective-permute-start(bf16[2,4,160,640]{3,2,1,0:T(8,128)(2,1)} %pad_maximum_fusion.1.own), channel_id=1, source_target_pairs={{0,4},{1,5},{2,6},{3,7},{4,0},{5,1},{6,2},{7,3},{8,12},{9,13},{10,... | collective-permute-start | bytes 4915208 | tf_op jit(solution)/shard_map/ppermute | solution.py:67
  934.2 47.4 %collective-permute-start.89 = (bf16[2,4,160,640]{3,2,1,0:T(8,128)(2,1)S(1)}, bf16[2,4,160,640]{3,2,1,0:T(8,128)(2,1)S(1)}, u32[]{:S(2)}, u32[]{:S(2)}) collective-permute-start(bf16[2,4,160,640]{3,2,1,0:T(8,128)(2,1)S(1)} %pad_maximum_fusion.own), channel_id=1, source_target_pairs={{0,1},{1,0},{2,3},{3,2},{4,5},{5,4},{6,7},{7,6},{8,9},{9,8},{10,11... | collective-permute-start | bytes 4915208 | tf_op jit(solution)/shard_map/ppermute | solution.py:67
  934.2 48.6 %collective-permute-start.91 = (bf16[2,4,160,640]{3,2,1,0:T(8,128)(2,1)}, bf16[2,4,160,640]{3,2,1,0:T(8,128)(2,1)S(1)}, u32[]{:S(2)}, u32[]{:S(2)}) collective-permute-start(bf16[2,4,160,640]{3,2,1,0:T(8,128)(2,1)} %pad_maximum_fusion.1.own), channel_id=1, source_target_pairs={{0,1},{1,0},{2,3},{3,2},{4,5},{5,4},{6,7},{7,6},{8,9},{9,8},{10,11... | collective-permute-start | bytes 4915208 | tf_op jit(solution)/shard_map/ppermute | solution.py:67
  934.7 50.1 %collective-permute-start.90 = (bf16[2,4,160,640]{3,2,1,0:T(8,128)(2,1)}, bf16[2,4,160,640]{3,2,1,0:T(8,128)(2,1)S(1)}, u32[]{:S(2)}, u32[]{:S(2)}) collective-permute-start(bf16[2,4,160,640]{3,2,1,0:T(8,128)(2,1)} %collective-permute-done.87.far), channel_id=1, source_target_pairs={{0,1},{1,0},{2,3},{3,2},{4,5},{5,4},{6,7},{7,6},{8,9},{9,8},{10,11... | collective-permute-start | bytes 4915208 | tf_op jit(solution)/shard_map/ppermute | solution.py:67
  934.7 52.8 %collective-permute-start.92 = (bf16[2,4,160,640]{3,2,1,0:T(8,128)(2,1)}, bf16[2,4,160,640]{3,2,1,0:T(8,128)(2,1)S(1)}, u32[]{:S(2)}, u32[]{:S(2)}) collective-permute-start(bf16[2,4,160,640]{3,2,1,0:T(8,128)(2,1)} %collective-permute-done.88.far), channel_id=1, source_target_pairs={{0,1},{1,0},{2,3},{3,2},{4,5},{5,4},{6,7},{7,6},{8,9},{9,8},{10,11... | collective-permute-start | bytes 4915208 | tf_op jit(solution)/shard_map/ppermute | solution.py:67
  967.4 64.1 %collective-permute-start.97 = (bf16[160,1280]{1,0:T(8,128)(2,1)}, bf16[160,1280]{1,0:T(8,128)(2,1)}, u32[]{:S(2)}, u32[]{:S(2)}) collective-permute-start(bf16[160,1280]{1,0:T(8,128)(2,1)} %get-tuple-element.506), channel_id=1, source_target_pairs={{0,8},{1,9},{2,10},{3,11},{4,12},{5,13},{6,14},{7,15},{8,0},{9,1},... | collective-permute-start | bytes 1228808 | tf_op jit(solution)/shard_map/ppermute | solution.py:67
  981.5 50.1 %collective-permute-start.98 = (bf16[160,1280]{1,0:T(8,128)(2,1)}, bf16[160,1280]{1,0:T(8,128)(2,1)S(1)}, u32[]{:S(2)}, u32[]{:S(2)}) collective-permute-start(bf16[160,1280]{1,0:T(8,128)(2,1)} %get-tuple-element.506), channel_id=1, source_target_pairs={{0,16},{1,17},{2,18},{3,19},{4,20},{5,21},{6,22},{7,23},{8,24},{9,... | collective-permute-start | bytes 1228808 | tf_op jit(solution)/shard_map/ppermute | solution.py:67
  982.8 49.3 %collective-permute-start.99 = (bf16[160,1280]{1,0:T(8,128)(2,1)}, bf16[160,1280]{1,0:T(8,128)(2,1)S(1)}, u32[]{:S(2)}, u32[]{:S(2)}) collective-permute-start(bf16[160,1280]{1,0:T(8,128)(2,1)} %get-tuple-element.506), channel_id=1, source_target_pairs={{0,24},{1,25},{2,26},{3,27},{4,28},{5,29},{6,30},{7,31},{8,16},{9,... | collective-permute-start | bytes 1228808 | tf_op jit(solution)/shard_map/ppermute | solution.py:67
  986.0 48.6 %collective-permute-start.95 = (bf16[2,4,40,2560]{3,2,1,0:T(8,128)(2,1)S(1)}, bf16[2,4,40,2560]{3,2,1,0:T(8,128)(2,1)}, u32[]{:S(2)}, u32[]{:S(2)}) collective-permute-start(bf16[2,4,40,2560]{3,2,1,0:T(8,128)(2,1)S(1)} %pad_maximum_fusion.2.own), channel_id=1, source_target_pairs={{0,2},{1,3},{2,0},{3,1},{4,6},{5,7},{6,4},{7,5},{8,10},{9,11},{10,... | collective-permute-start | bytes 4915208 | tf_op jit(solution)/shard_map/ppermute | solution.py:67
  988.7 45.9 %collective-permute-start.96 = (bf16[2,4,40,2560]{3,2,1,0:T(8,128)(2,1)}, bf16[2,4,40,2560]{3,2,1,0:T(8,128)(2,1)}, u32[]{:S(2)}, u32[]{:S(2)}) collective-permute-start(bf16[2,4,40,2560]{3,2,1,0:T(8,128)(2,1)} %pad_maximum_fusion.3.own), channel_id=1, source_target_pairs={{0,4},{1,5},{2,6},{3,7},{4,0},{5,1},{6,2},{7,3},{8,12},{9,13},{10,... | collective-permute-start | bytes 4915208 | tf_op jit(solution)/shard_map/ppermute | solution.py:67
  (139 other events, 2325.5 us)
